TPU v7x, 32 devices: a whole 2x2x4 slice. The times are simulated.
32 devices in a mesh: gx: 4 (over x, core), gy: 4 (over z), gz: 2 (over y).
Axes of the slice: x: 2, y: 2, z: 4, core: 2. Of those that a mesh axis runs over, the one named last changes fastest.
Arguments:
- fractions: float32 [4, 4, 2, 3, 256], P('gx', 'gy', 'gz'), may hold values from 0 to 1
- velocity: float32 [4, 4, 2, 3, 256], P('gx', 'gy', 'gz'), may hold values from -30 to 30
- charge: float32 [4, 4, 2, 256], P('gx', 'gy', 'gz'), may hold values from -1.5 to 1.5
- drude_charge: float32 [4, 4, 2, 256], P('gx', 'gy', 'gz'), may hold values from -2.2 to -0.8
- screening: float32 [4, 4, 2, 256], P('gx', 'gy', 'gz'), may hold values from 0.2 to 2
- labels: int32 [4, 4, 2, 256], P('gx', 'gy', 'gz'), may hold values from 0 to 255
- masses: float32 [4, 4, 2, 256], P('gx', 'gy', 'gz'), may hold values from 4 to 32
- counts: int32 [4, 4, 2], P('gx', 'gy', 'gz'), may hold values from 128 to 256, as said below
- leaving: int32 [4, 4, 2, 6, 16], P('gx', 'gy', 'gz'), may hold values from -1 to 255, as said below
Outputs:
- staying: float32 [4, 4, 2, 9, 256], P('gx', 'gy', 'gz')
- arrivals: float32 [4, 4, 2, 14, 96], P('gx', 'gy', 'gz')
Inputs may be any that keep to these rules, and one draw needn't show every extreme that they name: `counts`: at least one box holds 256 atoms. `leaving`: entries name distinct live slots of their box, or are -1; in every box some face has all 16 entries used.
All inputs are finite; a program needn't handle non-finite values.
Results may differ from a plain program's by a relative error of at most 0.0003.
Values sent between devices are 32-bit elements; how exact they have to be, the bound alone decides.
No kernel may reach another device: no remote copies, remote signals or barrier semaphores. Data moves between devices by JAX's collectives and lax.ppermute only.
A program may use at most 64 MiB of HBM per device.

v0:
```python
import itertools

import jax
import jax.numpy as jnp
import numpy as np
from jax import lax
from jax.experimental import pallas as pl
from jax.experimental.pallas import tpu as pltpu
from jax.sharding import PartitionSpec as P

ITERS = 3
CUTOFF = 12.0
DRUDE_GAIN = 0.3320636
KICK = 0.002 * 418.4 * 332.0636
TIMESTEP = 0.002
UNITS = ((1, 0, 0), (-1, 0, 0), (0, 1, 0), (0, -1, 0), (0, 0, 1), (0, 0, -1))
AXES = ("gx", "gy", "gz")
LANES = 128
CENTERS = ((0, 0, 0),) + tuple(tuple(-step for step in unit) for unit in UNITS)
MOMENT = 2.0 / CUTOFF**3
F32 = jnp.float32
HIGHEST = lax.Precision.HIGHEST
VMEM = pltpu.VMEM


def vmem():
    return pl.BlockSpec(memory_space=pltpu.VMEM)


def smem():
    return pl.BlockSpec(memory_space=pltpu.SMEM)


def anywhere():
    return pl.BlockSpec(memory_space=pltpu.HBM)


def box_length(slots):
    return max(12.0, (10.0 * slots) ** (1.0 / 3.0))


def axis_steps(count):
    return ((0, False), (1, True)) if count == 2 else ((-1, False), (0, False), (1, False))


def shell(sizes):
    return list(itertools.product(*[axis_steps(count) for count in sizes]))


def own_cell():
    return [lax.axis_index(axis) for axis in AXES]


def linear(cell, steps, sizes):
    value = 0
    for coordinate, step, count in zip(cell, steps, sizes):
        value = value * count + (coordinate + (step % count)) % count
    return value


def around(cell, center, boxes, sizes):
    return [linear(cell, [center[a] + box[a][0] for a in range(3)], sizes) for box in boxes]


def fill_table(table, cell, boxes, sizes):
    for g, center in enumerate(CENTERS):
        for n, place in enumerate(around(cell, center, boxes, sizes)):
            table[g * len(boxes) + n] = place


def row_dot(rows, hit):
    return jnp.dot(rows, hit, precision=HIGHEST, preferred_element_type=F32)


def pack_kernel(sizes, slots, moves):
    devices = int(np.prod(sizes))

    def kernel(*refs):
        count, inputs, (send, own), staged, sems = refs[0], refs[1:9], refs[9:11], refs[11:19], refs[19]
        copies = [pltpu.make_async_copy(inputs[i], staged[i], sems.at[i]) for i in range(8)]
        for copy in copies:
            copy.start()
        for copy in copies:
            copy.wait()
        frac, vel, charge, drude, screen, label, mass, leaving = staged
        cell = own_cell()
        lane = lax.broadcasted_iota(jnp.int32, (1, slots), 1)
        live = lane < count[0]
        fr = jnp.concatenate([frac[a] for a in range(3)], axis=0)
        ve = jnp.concatenate([vel[a] for a in range(3)], axis=0)
        q = jnp.where(live, charge[...], 0.0)
        qd = jnp.where(live, drude[...], -1.0)
        sc = screen[...]
        lb = label[...].astype(F32)
        ms = mass[...]
        lv = jnp.concatenate([leaving[k].astype(F32) for k in range(6)], axis=0)
        lv = jnp.concatenate([lv, jnp.full((2, moves), -1.0, F32)], axis=0)
        spread = (
            lax.broadcasted_iota(jnp.int32, (moves, LANES), 1) % moves
            == lax.broadcasted_iota(jnp.int32, (moves, LANES), 0)
        ).astype(F32)
        repeated = row_dot(lv, spread)
        slot_col = lax.broadcasted_iota(jnp.int32, (slots, LANES), 0).astype(F32)
        values = jnp.concatenate([ve, ms, jnp.zeros((4, slots), F32)], axis=0)
        field = lax.broadcasted_iota(jnp.int32, (8, LANES), 1) // moves - 1
        wanted = field == lax.broadcasted_iota(jnp.int32, (8, LANES), 0)
        first = lax.broadcasted_iota(jnp.int32, (1, LANES), 1) < moves
        departed = jnp.zeros((1, slots), F32)
        statics = jnp.concatenate([fr, q, qd, sc, lb, jnp.zeros((1, slots), F32)], axis=0)
        send[...] = jnp.broadcast_to(statics[None], (devices, 8, slots))
        ones = jnp.ones((8, LANES), jnp.bfloat16)
        for k, unit in enumerate(UNITS):
            hit = slot_col == repeated[k : k + 1]
            picked = row_dot(values, hit.astype(F32))
            row = jnp.sum(jnp.where(wanted, picked, 0.0), axis=0, keepdims=True)
            row = jnp.where(first, repeated[k : k + 1], row)
            side = (k % 2) * LANES
            send[linear(cell, unit, sizes), 7:8, side : side + LANES] = row
            departed = departed + lax.dot_general(
                ones,
                hit.astype(F32).astype(jnp.bfloat16),
                (((1,), (1,)), ((), ())),
                preferred_element_type=F32,
            )[0:1]
        alive = live.astype(F32)
        gain = jnp.where(live, DRUDE_GAIN * qd, 0.0)
        own[...] = jnp.concatenate(
            [fr, q, qd, sc, lb, ms, ve, alive, jnp.where(departed > 0.5, 0.0, alive)]
            + [MOMENT * (gain * qd), gain, KICK * q / ms],
            axis=0,
        )

    return kernel


def columns(rows):
    lanes = rows.shape[1]
    padded = jnp.concatenate([rows, jnp.zeros((LANES - rows.shape[0], lanes), F32)], axis=0)
    return padded.T


def derived(fr, qd, sc, length):
    root = (DRUDE_GAIN**-0.5) / jnp.abs(qd)
    return fr * length, root, (0.25 * CUTOFF**3) * sc * root


def target_of(block, length, count):
    rows = block.shape[0]
    wide = [jnp.broadcast_to(block[:, c : c + 1], (rows, LANES)) for c in range(count)]
    shifted = [{-1: wide[a] + length, 0: wide[a], 1: wide[a] - length} for a in range(3)]
    return wide, shifted


def reader(source, place, half, rows):
    lanes = slice(half * LANES, (half + 1) * LANES)
    return lambda c: jnp.broadcast_to(source[place, c : c + 1, lanes], (rows, LANES))


def offsets(wide, shifted, row, box, length):
    deltas = []
    for a in range(3):
        step, nearest = box[a]
        if nearest:
            raw = wide[a] - row(a)
            deltas.append(raw - jnp.where(raw > 0.0, length, -length))
        else:
            deltas.append(shifted[a][step] - row(a))
    return deltas


def norm(deltas):
    return deltas[0] * deltas[0] + deltas[1] * deltas[1] + deltas[2] * deltas[2]


def terms(wide, dist_sq, row):
    inverse = lax.rsqrt(dist_sq)
    fade = inverse * jnp.maximum(1.0 - dist_sq, 0.0)
    half_x = (wide[3] * row(5) + wide[4] * row(4)) * (dist_sq * (dist_sq * inverse))
    tanh = jnp.tanh(half_x)
    root = lax.rsqrt(1.0 + tanh)
    base = ((fade * fade) * inverse) * (root * root)
    return inverse, half_x, tanh, base


def charge_sum(fields, wide, deltas, direct, row):
    weight = jnp.where(wide[5] != row(6), direct, 0.0) * row(3)
    return [fields[a] + weight * deltas[a] for a in range(3)]


def is_center(box):
    return all(step == 0 for step, _ in box)


def rows_of(parts):
    return [jnp.sum(part.T, axis=0, keepdims=True) for part in parts]


def send_moments(send, moments, slots):
    rows = [m[:, h * LANES : (h + 1) * LANES] for m in moments for h in range(slots // LANES)]
    rows.append(jnp.zeros((send.shape[1] - len(rows), LANES), F32))
    block = jnp.concatenate(rows, axis=0)
    send[...] = jnp.broadcast_to(block[None], send.shape)


def charge_kernel(sizes, slots, tile):
    boxes = shell(sizes)
    length = box_length(slots) / CUTOFF

    def kernel(recv, own, source, cols, perm, send, acc):
        fr, root, part = derived(recv[:, 0:3, :], recv[:, 4:5, :], recv[:, 5:6, :], length)
        source[:, 0:3, :] = fr
        source[:, 3:4, :] = (2.0 / CUTOFF**2) * recv[:, 3:4, :]
        source[:, 4:5, :] = root
        source[:, 5:6, :] = part
        source[:, 6:8, :] = recv[:, 6:8, :]
        fr, root, part = derived(own[0:3], own[4:5], own[5:6], length)
        ident = lax.broadcasted_iota(jnp.int32, (1, slots), 1).astype(F32)
        cols[...] = columns(jnp.concatenate([fr, root, part, own[6:7], ident, ident], axis=0))
        places = around(own_cell(), CENTERS[0], boxes, sizes)

        def body(t, carry):
            at = pl.ds(pl.multiple_of(t * tile, tile), tile)
            wide, shifted = target_of(cols[at, :], length, 6)
            fields = [jnp.zeros((tile, LANES), F32)] * 3
            for n, box in enumerate(boxes):
                for half in range(slots // LANES):
                    row = reader(source, places[n], half, tile)
                    deltas = offsets(wide, shifted, row, box, length)
                    _, _, tanh, base = terms(wide, norm(deltas), row)
                    fields = charge_sum(fields, wide, deltas, base * tanh, row)
            for a in range(3):
                acc[a, at, :] = fields[a]
            return carry

        lax.fori_loop(0, slots // tile, body, 0)
        rows = rows_of([acc[a] for a in range(3)])
        perm[...] = jnp.concatenate(rows, axis=0)
        send_moments(send, [own[13:14] * row for row in rows], slots)

    return kernel


def tensor_kernel(sizes, slots, moves):
    boxes = shell(sizes)
    length = box_length(slots) / CUTOFF
    tile = moves
    near_tiles = slots // tile

    def kernel(recv, source, cols, pairs, arrive, hits, perm, cols_in, stage, acc, table, sems):
        cell = own_cell()
        fill_table(table, cell, boxes, sizes)
        lane = lax.broadcasted_iota(jnp.int32, (1, LANES), 1)
        origin = [linear(cell, [-step for step in unit], sizes) for unit in UNITS]
        extra = jnp.full((8, LANES), -1.0, F32)
        for k in range(6):
            side = (k % 2) * LANES
            row = recv[origin[k], 7:8, side : side + LANES]
            row = jnp.broadcast_to(row, (8, LANES))
            fields = [pltpu.roll(row, (k * moves - c * moves) % LANES, 1)[0:1] for c in range(5)]
            block = jnp.concatenate(fields + [extra[0:3]], axis=0)
            extra = jnp.where(lane // moves == k, block, extra)
        slot = extra[0:1]
        slot_col = lax.broadcasted_iota(jnp.int32, (slots, LANES), 0).astype(F32)
        hit = (slot_col == slot).astype(F32)
        hits[...] = hit
        got = jnp.zeros((8, LANES), F32)
        for k in range(6):
            got = jnp.where(lane // moves == k, row_dot(recv[origin[k]], hit), got)
        present = (slot >= 0.0).astype(F32)
        arrive[...] = jnp.concatenate([got[0:7], extra[4:5], extra[1:4], present, slot, extra[5:8]], axis=0)
        fr, root, part = derived(got[0:3], got[4:5] - (1.0 - present), got[5:6], length)
        cols_in[...] = columns(jnp.concatenate([fr, root, part, got[6:7], slot, slot], axis=0))

        def body(t, block, offset, charges):
            wide, shifted = target_of(block, length, 7)
            fields = [jnp.zeros((tile, LANES), F32)] * 3
            for n, box in enumerate(boxes):
                place = table[offset + n]
                for half in range(slots // LANES):
                    row = reader(source, place, half, tile)
                    deltas = offsets(wide, shifted, row, box, length)
                    dist_sq = norm(deltas)
                    keep = None
                    if is_center(box):
                        ids = lax.broadcasted_iota(jnp.int32, (tile, LANES), 1) + half * LANES
                        keep = wide[6] != ids.astype(F32)
                        dist_sq = jnp.where(keep, dist_sq, 1.0)
                    inverse, half_x, tanh, base = terms(wide, dist_sq, row)
                    direct = base * tanh
                    if charges:
                        fields = charge_sum(fields, wide, deltas, direct, row)
                    radial = (base * (3.0 * inverse)) * (inverse * (tanh - half_x * (1.0 - tanh)))
                    if keep is not None:
                        direct = jnp.where(keep, direct, 0.0)
                        radial = jnp.where(keep, radial, 0.0)
                    lanes = slice(n * slots + half * LANES, n * slots + (half + 1) * LANES)
                    stage[t, 0, :, lanes] = radial
                    stage[t, 1, :, lanes] = direct
            pltpu.make_async_copy(stage.at[t], pairs.at[t], sems.at[t]).start()
            return fields

        def near(t, carry):
            body(t, cols[pl.ds(pl.multiple_of(t * tile, tile), tile), :], 0, False)
            return carry

        def incoming(k, carry):
            at = pl.ds(pl.multiple_of(k * tile, tile), tile)
            fields = body(near_tiles + k, cols_in[at, :], (k + 1) * len(boxes), True)
            for a in range(3):
                acc[a, at, :] = fields[a]
            return carry

        acc[...] = jnp.zeros(acc.shape, F32)
        lax.fori_loop(0, near_tiles, near, 0)
        lax.fori_loop(0, 6, incoming, 0)
        perm[...] = jnp.concatenate(rows_of([acc[a] for a in range(3)]), axis=0)

        def settle(t, carry):
            pltpu.make_async_copy(stage.at[t], pairs.at[t], sems.at[t]).wait()
            return carry

        lax.fori_loop(0, near_tiles + 6, settle, 0)

    return kernel


def apply_tile(block, load, source, recv, place_of, boxes, slots, length):
    rows = block.shape[0]
    halves = slots // LANES
    wide, shifted = target_of(block, length, 3)
    fields = [jnp.zeros((rows, LANES), F32)] * 3
    for n, box in enumerate(boxes):
        place = place_of(n)
        for half in range(halves):
            lanes = slice(n * slots + half * LANES, n * slots + (half + 1) * LANES)
            mu = [
                jnp.broadcast_to(recv[place, a * halves + half : a * halves + half + 1, :], (rows, LANES))
                for a in range(3)
            ]
            deltas = offsets(wide, shifted, reader(source, place, half, rows), box, length)
            along = load(0, lanes) * (deltas[0] * mu[0] + deltas[1] * mu[1] + deltas[2] * mu[2])
            direct = load(1, lanes)
            fields = [fields[a] + (along * deltas[a] - direct * mu[a]) for a in range(3)]
    return fields


def induced_kernel(sizes, slots, tile, fetch):
    boxes = shell(sizes)
    length = box_length(slots) / CUTOFF
    tiles = slots // tile

    def kernel(recv, pairs, source, cols, own, perm, send, shift, *rest):
        if fetch:
            kept, acc, sems = rest

            def begin(t, carry):
                pltpu.make_async_copy(pairs.at[t], kept.at[t], sems.at[t]).start()
                return carry

            lax.fori_loop(0, tiles, begin, 0)
        else:
            (acc,) = rest
            kept = pairs
        places = around(own_cell(), CENTERS[0], boxes, sizes)

        def body(t, carry):
            if fetch:
                pltpu.make_async_copy(pairs.at[t], kept.at[t], sems.at[t]).wait()
            at = pl.ds(pl.multiple_of(t * tile, tile), tile)
            load = lambda which, lanes: kept[t, which, :, lanes]
            fields = apply_tile(cols[at, :], load, source, recv, lambda n: places[n], boxes, slots, length)
            for a in range(3):
                acc[a, at, :] = fields[a]
            return carry

        lax.fori_loop(0, tiles, body, 0)
        rows = rows_of([acc[a] for a in range(3)])
        rows = [rows[a] + perm[a : a + 1] for a in range(3)]
        shift[...] = jnp.concatenate([own[14:15] * row for row in rows], axis=0)
        send_moments(send, [own[13:14] * row for row in rows], slots)

    return kernel


def final_kernel(sizes, slots, moves):
    boxes = shell(sizes)
    tile = moves
    halves = slots // LANES
    tiles = slots // tile
    edge = box_length(slots)
    length = edge / CUTOFF

    def kernel(
        recv, pairs, far, source, cols, own, perm, shift, arrive, hits, perm_in, cols_in,
        staying, arrivals, acc, kept, table, out_stay, out_come, sems, out_sems,
    ):
        def begin(k, carry):
            pltpu.make_async_copy(far.at[tiles + k], kept.at[k], sems.at[k]).start()
            return carry

        lax.fori_loop(0, 6, begin, 0)
        cell = own_cell()
        fill_table(table, cell, boxes, sizes)
        acc[...] = jnp.zeros(acc.shape, F32)
        lane = lax.broadcasted_iota(jnp.int32, (1, LANES), 1)

        def body(t, carry):
            at = pl.ds(pl.multiple_of(t * tile, tile), tile)
            load = lambda which, lanes: pairs[t, which, :, lanes]
            fields = apply_tile(cols[at, :], load, source, recv, lambda n: table[n], boxes, slots, length)
            for a in range(3):
                acc[a, at, :] = fields[a]
            return carry

        lax.fori_loop(0, tiles, body, 0)

        def incoming(k, carry):
            pltpu.make_async_copy(far.at[tiles + k], kept.at[k], sems.at[k]).wait()
            at = pl.ds(pl.multiple_of(k * tile, tile), tile)
            load = lambda which, lanes: kept[k, which, :, lanes]
            place_of = lambda n: table[(k + 1) * len(boxes) + n]
            fields = apply_tile(cols_in[at, :], load, source, recv, place_of, boxes, slots, length)
            for a in range(3):
                acc[a, pl.ds(pl.multiple_of(slots + k * tile, tile), tile), :] = fields[a]
            return carry

        lax.fori_loop(0, 6, incoming, 0)
        sums = rows_of([acc[a] for a in range(3)])
        field = [sums[a][:, 0:slots] + perm[a : a + 1] for a in range(3)]
        remain = own[12:13] > 0.5
        fast = [own[8 + a : 9 + a] + own[15:16] * field[a] for a in range(3)]
        place = [own[a : a + 1] + TIMESTEP * fast[a] / edge for a in range(3)]
        drude = [shift[a : a + 1] for a in range(3)]
        for r, row in enumerate(place + fast + drude):
            out_stay[r] = jnp.where(remain, row, 0.0)
        first = pltpu.make_async_copy(out_stay, staying, out_sems.at[0])
        first.start()

        moment = jnp.zeros((8, LANES), F32)
        for k, unit in enumerate(UNITS):
            block = recv[linear(cell, [-step for step in unit], sizes)]
            both = [row_dot(block, hits[h * LANES : (h + 1) * LANES, :]) for h in range(halves)]
            one = [
                sum(both[h][a * halves + h : a * halves + h + 1] for h in range(halves)) for a in range(3)
            ]
            one = jnp.concatenate(one + [jnp.zeros((5, LANES), F32)], axis=0)
            moment = jnp.where(lane // moves == k, one, moment)
        present = arrive[11:12] > 0.5
        q = arrive[3:4]
        qd = arrive[4:5]
        mass = jnp.where(present, arrive[7:8], 1.0)
        gain = KICK * q / mass
        pull = [sums[a][:, slots : slots + LANES] + perm_in[a : a + 1] for a in range(3)]
        fast = [arrive[8 + a : 9 + a] + gain * pull[a] for a in range(3)]
        place = [arrive[a : a + 1] + TIMESTEP * fast[a] / edge for a in range(3)]
        for k, unit in enumerate(UNITS):
            for a in range(3):
                if unit[a]:
                    place[a] = place[a] - jnp.where(lane // moves == k, float(unit[a]), 0.0)
        safe = jnp.where(present, qd, -1.0) * MOMENT
        drude = [moment[a : a + 1] / safe for a in range(3)]
        record = place + fast + drude + [q, qd, arrive[5:6], arrive[6:7], mass]
        for r, row in enumerate(record):
            out_come[r] = jnp.where(present, row, 0.0)[:, 0 : 6 * moves]
        second = pltpu.make_async_copy(out_come, arrivals, out_sems.at[1])
        second.start()
        first.wait()
        second.wait()

    return kernel


def solution(mesh):
    sizes = tuple(mesh.shape[axis] for axis in AXES)
    devices = int(np.prod(sizes))
    count_boxes = len(shell(sizes))

    def local(fractions, velocity, charge, drude_charge, screening, labels, masses, counts, leaving):
        slots = charge.shape[-1]
        moves = leaving.shape[-1]
        tiles = slots // moves
        lanes = count_boxes * slots
        exchange = lambda block: lax.all_to_all(block, AXES, 0, 0)
        shape = lambda *dims: jax.ShapeDtypeStruct(dims, F32)
        hbm = lambda x: pltpu.with_memory_space_constraint(x, pltpu.HBM)
        moment_shape = (devices, 8, LANES)
        dma = pltpu.SemaphoreType.DMA

        def call(kernel, in_specs, outs, out_specs, scratch, flops, limit):
            return pl.pallas_call(
                kernel,
                in_specs=in_specs,
                out_shape=outs,
                out_specs=out_specs,
                scratch_shapes=scratch,
                compiler_params=pltpu.CompilerParams(vmem_limit_bytes=limit),
                cost_estimate=pl.CostEstimate(flops=flops, bytes_accessed=1 << 20, transcendentals=0),
            )

        flat = [
            fractions.reshape(3, 1, slots),
            velocity.reshape(3, 1, slots),
            charge.reshape(1, slots),
            drude_charge.reshape(1, slots),
            screening.reshape(1, slots),
            labels.reshape(1, slots),
            masses.reshape(1, slots),
            leaving.reshape(6, 1, moves),
        ]
        send, own = call(
            pack_kernel(sizes, slots, moves),
            [smem()] + [anywhere()] * 8,
            (shape(devices, 8, slots), shape(16, slots)),
            (vmem(), vmem()),
            [VMEM(array.shape, array.dtype) for array in flat] + [dma((8,))],
            1 << 20,
            8 << 20,
        )(counts.reshape(1), *[hbm(x) for x in flat])
        recv = exchange(send)
        source, cols, perm, moments = call(
            charge_kernel(sizes, slots, moves),
            [vmem()] * 2,
            (shape(devices, 8, slots), shape(slots, LANES), shape(3, slots), shape(*moment_shape)),
            (vmem(),) * 4,
            [VMEM((3, slots, LANES), F32)],
            1 << 25,
            8 << 20,
        )(recv, own)
        got = exchange(moments)
        pairs, arrive, hits, perm_in, cols_in = call(
            tensor_kernel(sizes, slots, moves),
            [vmem()] * 3,
            (
                pltpu.HBM((tiles + 6, 2, moves, lanes), F32),
                shape(16, LANES),
                shape(slots, LANES),
                shape(3, LANES),
                shape(LANES, LANES),
            ),
            (anywhere(),) + (vmem(),) * 4,
            [
                VMEM((tiles + 6, 2, moves, lanes), F32),
                VMEM((3, LANES, LANES), F32),
                pltpu.SMEM((len(CENTERS) * count_boxes,), jnp.int32),
                dma((tiles + 6,)),
            ],
            1 << 26,
            32 << 20,
        )(recv, source, cols)
        far = pairs
        acc = VMEM((3, slots, LANES), F32)
        for step in range(ITERS - 1):
            outs = (shape(*moment_shape), shape(3, slots))
            fetch = step == 0
            if fetch:
                outs = outs + (shape(tiles, 2, moves, lanes),)
            results = call(
                induced_kernel(sizes, slots, moves, fetch),
                [vmem(), anywhere() if fetch else vmem()] + [vmem()] * 4,
                outs,
                (vmem(),) * len(outs),
                [acc, dma((tiles,))] if fetch else [acc],
                1 << 24,
                4 << 20,
            )(got, hbm(pairs) if fetch else pairs, source, cols, own, perm)
            moments, shift = results[:2]
            if fetch:
                pairs = results[2]
            got = exchange(moments)
        staying, arrivals = call(
            final_kernel(sizes, slots, moves),
            [vmem(), vmem(), anywhere()] + [vmem()] * 9,
            (pltpu.HBM((9, 1, slots), F32), pltpu.HBM((14, 1, 6 * moves), F32)),
            (anywhere(), anywhere()),
            [
                VMEM((3, slots + LANES, LANES), F32),
                VMEM((6, 2, moves, lanes), F32),
                pltpu.SMEM((len(CENTERS) * count_boxes,), jnp.int32),
                VMEM((9, 1, slots), F32),
                VMEM((14, 1, 6 * moves), F32),
                dma((6,)),
                dma((2,)),
            ],
            1 << 24,
            16 << 20,
        )(got, pairs, hbm(far), source, cols, own, perm, shift, arrive, hits, perm_in, cols_in)
        return staying.reshape(1, 1, 1, 9, slots), arrivals.reshape(1, 1, 1, 14, 6 * moves)

    box = P("gx", "gy", "gz", None)
    rows = P("gx", "gy", "gz", None, None)
    return jax.shard_map(
        local,
        mesh=mesh,
        in_specs=(rows, rows, box, box, box, box, box, P("gx", "gy", "gz"), rows),
        out_specs=(rows, rows),
        check_vma=False,
    )
```

profile of v0, /device:TPU:0, one launch (start us, length us, event | category | flops | bytes accessed | tf_op | source)
XLA Modules:
  0.0 85.9 jit_solution(2849470220667286702)
XLA Ops:
  1.3 1.6 %shard_map.104 = (f32[32,8,256]{2,1,0:T(8,128)S(1)}, f32[16,256]{1,0:T(8,128)S(1)}) custom-call(s32[1]{0:T(128)} %bitcast.15.refs_0_, f32[3,1,256]{2,1,0:T(1,128)} %bitcast.16, f32[3,1,256]{2,1,0:T(1,128)} %bitcast.17, f32[1,256]{1,0:T(1,128)} %bitcast.19, f32[1,256]{1,0:T(1,128)} %bitcast.20, f32[1,256]{1,0:T(1,128)} %bitcast.21, s32[1,256]{1,0:T(1,128)} %bitcast.22, ...), custom_call_target="tpu_custom_call" | custom-call | flops 1048576 | bytes 1048576 | tf_op jit(solution)/shard_map/pallas_call | solution.py:510
  2.8 17.6 %all_to_all.20.recv = f32[32,8,256]{2,1,0:T(8,128)S(1)} all-to-all(f32[32,8,256]{2,1,0:T(8,128)S(1)} %get-tuple-element.19), channel_id=1, replica_groups=mesh['gx'=4,'gy'=4,'gz'=2] {'gx','gy','gz'}, dimensions={0} | all-to-all | bytes 524288 | tf_op jit(solution)/shard_map/all_to_all | solution.py:483
  20.4 8.0 %shard_map.105 = (f32[32,8,256]{2,1,0:T(8,128)S(1)}, f32[256,128]{1,0:T(8,128)S(1)}, f32[3,256]{1,0:T(4,128)S(1)}, f32[32,8,128]{2,1,0:T(8,128)}) custom-call(f32[32,8,256]{2,1,0:T(8,128)S(1)} %all_to_all.20.recv, f32[16,256]{1,0:T(8,128)S(1)} %get-tuple-element.20.own), custom_call_target="tpu_custom_call" | custom-call | flops 33554432 | bytes 1048576 | tf_op jit(solution)/shard_map/pallas_call | solution.py:520
  28.4 2.6 %all-to-all-start.1 = ((f32[32,8,128]{2,1,0:T(8,128)}), f32[32,8,128]{2,1,0:T(8,128)S(1)}, u32[]{:S(2)}, u32[]{:S(2)}) async-start(f32[32,8,128]{2,1,0:T(8,128)} %get-tuple-element.21), calls=%async_computation.1 | async-start | bytes 262144 | tf_op jit(solution)/shard_map/all_to_all | solution.py:483
  31.0 11.6 %shard_map.106 = (f32[22,2,16,4608]{3,2,1,0:T(8,128)}, f32[16,128]{1,0:T(8,128)S(1)}, f32[256,128]{1,0:T(8,128)S(1)}, f32[3,128]{1,0:T(4,128)S(1)}, f32[128,128]{1,0:T(8,128)S(1)}) custom-call(f32[32,8,256]{2,1,0:T(8,128)S(1)} %all_to_all.20.recv, f32[32,8,256]{2,1,0:T(8,128)S(1)} %get-tuple-element.22.source, f32[256,128]{1,0:T(8,128)S(1)} %get-tuple-element.23.cols), custom_call_target="tpu_custom_call" | custom-call | flops 67108864 | bytes 1048576 | tf_op jit(solution)/shard_map/pallas_call | solution.py:530
  42.6 0.0 all-to-all-done.1.recv
  42.6 6.9 %shard_map.107 = (f32[32,8,128]{2,1,0:T(8,128)S(1)}, f32[3,256]{1,0:T(4,128)}, f32[16,2,16,4608]{3,2,1,0:T(8,128)S(1)}) custom-call(f32[32,8,128]{2,1,0:T(8,128)S(1)} %all-to-all-done.1.recv, f32[22,2,16,4608]{3,2,1,0:T(8,128)} %get-tuple-element.24.pairs.far, f32[32,8,256]{2,1,0:T(8,128)S(1)} %get-tuple-element.22.source, ...), custom_call_target="tpu_custom_call" | custom-call | flops 16777216 | bytes 1048576 | tf_op jit(solution)/shard_map/pallas_call | solution.py:557
  49.5 13.3 %all_to_all.21.recv = f32[32,8,128]{2,1,0:T(8,128)S(1)} all-to-all(f32[32,8,128]{2,1,0:T(8,128)S(1)} %get-tuple-element.26), channel_id=1, replica_groups=mesh['gx'=4,'gy'=4,'gz'=2] {'gx','gy','gz'}, dimensions={0} | all-to-all | bytes 262144 | tf_op jit(solution)/shard_map/all_to_all | solution.py:483
  62.8 5.1 %shard_map.108 = (f32[32,8,128]{2,1,0:T(8,128)S(1)}, f32[3,256]{1,0:T(4,128)S(1)}) custom-call(f32[32,8,128]{2,1,0:T(8,128)S(1)} %all_to_all.21.recv, f32[16,2,16,4608]{3,2,1,0:T(8,128)S(1)} %get-tuple-element.27.pairs, f32[32,8,256]{2,1,0:T(8,128)S(1)} %get-tuple-element.22.source, f32[256,128]{1,0:T(8,128)S(1)} %get-tuple-element.23.cols, ...), custom_call_target="tpu_custom_call" | custom-call | flops 16777216 | bytes 1048576 | tf_op jit(solution)/shard_map/pallas_call | solution.py:557
  67.9 10.0 %all_to_all.22.recv = f32[32,8,128]{2,1,0:T(8,128)S(1)} all-to-all(f32[32,8,128]{2,1,0:T(8,128)S(1)} %get-tuple-element.28), channel_id=1, replica_groups=mesh['gx'=4,'gy'=4,'gz'=2] {'gx','gy','gz'}, dimensions={0} | all-to-all | bytes 262144 | tf_op jit(solution)/shard_map/all_to_all | solution.py:483
  77.9 8.0 %shard_map.109 = (f32[9,1,256]{2,1,0:T(1,128)}, f32[14,1,96]{2,1,0:T(1,128)}) custom-call(f32[32,8,128]{2,1,0:T(8,128)S(1)} %all_to_all.22.recv, f32[16,2,16,4608]{3,2,1,0:T(8,128)S(1)} %get-tuple-element.27.pairs, f32[22,2,16,4608]{3,2,1,0:T(8,128)} %get-tuple-element.24.pairs.far, f32[32,8,256]{2,1,0:T(8,128)S(1)} %get-tuple-element.22.source, ...), custom_call_target="tpu_custom_call" | custom-call | flops 16777216 | bytes 1048576 | tf_op jit(solution)/shard_map/pallas_call | solution.py:570
Async XLA Ops:
  28.4 14.2 %all-to-all-start.1 = ((f32[32,8,128]{2,1,0:T(8,128)}), f32[32,8,128]{2,1,0:T(8,128)S(1)}, u32[]{:S(2)}, u32[]{:S(2)}) async-start(f32[32,8,128]{2,1,0:T(8,128)} %get-tuple-element.21), calls=%async_computation.1 | async-start | bytes 262144 | tf_op jit(solution)/shard_map/all_to_all | solution.py:483
where the time goes:
time: 86.1 us; the launch traced here: 85.9 us
  Pallas kernels  41.1 us (48%)
  blocking collectives  40.9 us (48%)
  starting transfers between devices  2.55 us (3%)
  between operations  1.33 us (2%)
    all_to_all x3, blocking collectives, local(): exchange = lambda block: lax.all_to_all(block, AXES, 0, 0)  40.9 us
    pallas_call x2, Pallas kernels, local(): call(induced_kernel(sizes, slots, moves, fetch), [vmem(), anywhere() if f...  12 us
    pallas_call x1, Pallas kernels, local(): call(tensor_kernel(sizes, slots, moves), [vmem()] * 3, (pltpu.HBM((tiles...  11.6 us
    pallas_call x1, Pallas kernels, local(): call(charge_kernel(sizes, slots, moves), [vmem()] * 2, (shape(devices, 8,...  8 us
    pallas_call x1, Pallas kernels, local(): call(final_kernel(sizes, slots, moves), [vmem(), vmem(), anywhere()] + [v...  7.97 us
    all_to_all x1, starting transfers between devices, local(): exchange = lambda block: lax.all_to_all(block, AXES, 0, 0)  2.55 us
  transfers between devices with their start and end apart: 1, of which 0 were waited for; matrix products, arithmetic and copies ran while one was open for 0% of the time, Pallas kernels for 13%

commit v1 on v0

v1 whole, which is shorter than its diff:
```python
import itertools

import jax
import jax.numpy as jnp
import numpy as np
from jax import lax
from jax.experimental import pallas as pl
from jax.experimental.pallas import tpu as pltpu
from jax.sharding import PartitionSpec as P

ITERS = 3
CUTOFF = 12.0
DRUDE_GAIN = 0.3320636
KICK = 0.002 * 418.4 * 332.0636
TIMESTEP = 0.002
UNITS = ((1, 0, 0), (-1, 0, 0), (0, 1, 0), (0, -1, 0), (0, 0, 1), (0, 0, -1))
AXES = ("gx", "gy", "gz")
LANES = 128
CENTERS = ((0, 0, 0),) + tuple(tuple(-step for step in unit) for unit in UNITS)
MOMENT = 2.0 / CUTOFF**3
F32 = jnp.float32
BF16 = jnp.bfloat16
HIGHEST = lax.Precision.HIGHEST
VMEM = pltpu.VMEM


def vmem():
    return pl.BlockSpec(memory_space=pltpu.VMEM)


def smem():
    return pl.BlockSpec(memory_space=pltpu.SMEM)


def anywhere():
    return pl.BlockSpec(memory_space=pltpu.HBM)


def box_length(slots):
    return max(12.0, (10.0 * slots) ** (1.0 / 3.0))


def axis_steps(count):
    return ((0, False), (1, True)) if count == 2 else ((-1, False), (0, False), (1, False))


def shell(sizes):
    return list(itertools.product(*[axis_steps(count) for count in sizes]))


def own_cell():
    return [lax.axis_index(axis) for axis in AXES]


def linear(cell, steps, sizes):
    value = 0
    for coordinate, step, count in zip(cell, steps, sizes):
        value = value * count + (coordinate + (step % count)) % count
    return value


def around(cell, center, boxes, sizes):
    return [linear(cell, [center[a] + box[a][0] for a in range(3)], sizes) for box in boxes]


def fill_table(table, cell, boxes, sizes):
    for g, center in enumerate(CENTERS):
        for n, place in enumerate(around(cell, center, boxes, sizes)):
            table[g * len(boxes) + n] = place


def row_dot(rows, hit):
    return jnp.dot(rows, hit, precision=HIGHEST, preferred_element_type=F32)


def pack_kernel(sizes, slots, moves):
    devices = int(np.prod(sizes))

    def kernel(*refs):
        count, inputs, (send, own), staged, sems = refs[0], refs[1:9], refs[9:11], refs[11:19], refs[19]
        copies = [pltpu.make_async_copy(inputs[i], staged[i], sems.at[i]) for i in range(8)]
        for copy in copies:
            copy.start()
        for copy in copies:
            copy.wait()
        frac, vel, charge, drude, screen, label, mass, leaving = staged
        cell = own_cell()
        lane = lax.broadcasted_iota(jnp.int32, (1, slots), 1)
        live = lane < count[0]
        fr = jnp.concatenate([frac[a] for a in range(3)], axis=0)
        ve = jnp.concatenate([vel[a] for a in range(3)], axis=0)
        q = jnp.where(live, charge[...], 0.0)
        qd = jnp.where(live, drude[...], -1.0)
        sc = screen[...]
        lb = label[...].astype(F32)
        ms = mass[...]
        lv = jnp.concatenate([leaving[k].astype(F32) for k in range(6)], axis=0)
        lv = jnp.concatenate([lv, jnp.full((2, moves), -1.0, F32)], axis=0)
        spread = (
            lax.broadcasted_iota(jnp.int32, (moves, LANES), 1) % moves
            == lax.broadcasted_iota(jnp.int32, (moves, LANES), 0)
        ).astype(F32)
        repeated = row_dot(lv, spread)
        slot_col = lax.broadcasted_iota(jnp.int32, (slots, LANES), 0).astype(F32)
        values = jnp.concatenate([ve, ms, jnp.zeros((4, slots), F32)], axis=0)
        field = lax.broadcasted_iota(jnp.int32, (8, LANES), 1) // moves - 1
        wanted = field == lax.broadcasted_iota(jnp.int32, (8, LANES), 0)
        first = lax.broadcasted_iota(jnp.int32, (1, LANES), 1) < moves
        departed = jnp.zeros((1, slots), F32)
        statics = jnp.concatenate([fr, q, qd, sc, lb, jnp.zeros((1, slots), F32)], axis=0)
        send[...] = jnp.broadcast_to(statics[None], (devices, 8, slots))
        ones = jnp.ones((8, LANES), BF16)
        for k, unit in enumerate(UNITS):
            hit = slot_col == repeated[k : k + 1]
            picked = row_dot(values, hit.astype(F32))
            row = jnp.sum(jnp.where(wanted, picked, 0.0), axis=0, keepdims=True)
            row = jnp.where(first, repeated[k : k + 1], row)
            side = (k % 2) * LANES
            send[linear(cell, unit, sizes), 7:8, side : side + LANES] = row
            departed = departed + lax.dot_general(
                ones,
                hit.astype(F32).astype(BF16),
                (((1,), (1,)), ((), ())),
                preferred_element_type=F32,
            )[0:1]
        alive = live.astype(F32)
        gain = jnp.where(live, DRUDE_GAIN * qd, 0.0)
        own[...] = jnp.concatenate(
            [fr, q, qd, sc, lb, ms, ve, alive, jnp.where(departed > 0.5, 0.0, alive)]
            + [MOMENT * (gain * qd), gain, KICK * q / ms],
            axis=0,
        )

    return kernel


def columns(rows):
    lanes = rows.shape[1]
    padded = jnp.concatenate([rows, jnp.zeros((LANES - rows.shape[0], lanes), F32)], axis=0)
    return padded.T


def derived(fr, qd, sc, length):
    root = (DRUDE_GAIN**-0.5) / jnp.abs(qd)
    return fr * length, root, (0.25 * CUTOFF**3) * sc * root


def target_of(block, length, count):
    rows = block.shape[0]
    wide = [jnp.broadcast_to(block[:, c : c + 1], (rows, LANES)) for c in range(count)]
    shifted = [{-1: wide[a] + length, 0: wide[a], 1: wide[a] - length} for a in range(3)]
    return wide, shifted


def reader(source, place, half, rows):
    lanes = slice(half * LANES, (half + 1) * LANES)
    return lambda c: jnp.broadcast_to(source[place, c : c + 1, lanes], (rows, LANES))


def offsets(wide, shifted, row, box, length):
    deltas = []
    for a in range(3):
        step, nearest = box[a]
        if nearest:
            raw = wide[a] - row(a)
            deltas.append(raw - jnp.where(raw > 0.0, length, -length))
        else:
            deltas.append(shifted[a][step] - row(a))
    return deltas


def norm(deltas):
    return deltas[0] * deltas[0] + deltas[1] * deltas[1] + deltas[2] * deltas[2]


def terms(wide, dist_sq, row):
    inverse = lax.rsqrt(dist_sq)
    fade = inverse * jnp.maximum(1.0 - dist_sq, 0.0)
    half_x = (wide[3] * row(5) + wide[4] * row(4)) * (dist_sq * (dist_sq * inverse))
    tanh = jnp.tanh(half_x)
    root = lax.rsqrt(1.0 + tanh)
    base = ((fade * fade) * inverse) * (root * root)
    return inverse, half_x, tanh, base


def charge_sum(fields, wide, deltas, direct, row):
    weight = jnp.where(wide[5] != row(6), direct, 0.0) * row(3)
    return [fields[a] + weight * deltas[a] for a in range(3)]


def image_list(boxes):
    first, rest = [], []
    for n, box in enumerate(boxes):
        combos = list(itertools.product(*[(1, -1) if nearest else (step,) for step, nearest in box]))
        first.append((n, combos[0]))
        rest.extend((n, combo) for combo in combos[1:])
    return first + rest


def is_center(box):
    return all(step == 0 for step, _ in box)


def rows_of(parts):
    return [jnp.sum(part.T, axis=0, keepdims=True) for part in parts]


def send_moments(send, moments, slots):
    rows = [m[:, h * LANES : (h + 1) * LANES] for m in moments for h in range(slots // LANES)]
    rows.append(jnp.zeros((send.shape[1] - len(rows), LANES), F32))
    block = jnp.concatenate(rows, axis=0)
    send[...] = jnp.broadcast_to(block[None], send.shape)


def split(values):
    high = values.astype(BF16)
    return high, (values - high.astype(F32)).astype(BF16)


def field_kernel(sizes, slots, tile):
    boxes = shell(sizes)
    images = image_list(boxes)
    length = box_length(slots) / CUTOFF

    def kernel(recv, own, source, frames, ahi, alo, bhi, blo, perm, send, chosen, cols, acc):
        fr, root, part = derived(recv[:, 0:3, :], recv[:, 4:5, :], recv[:, 5:6, :], length)
        source[:, 0:3, :] = fr
        source[:, 3:4, :] = (2.0 / CUTOFF**2) * recv[:, 3:4, :]
        source[:, 4:5, :] = root
        source[:, 5:6, :] = part
        source[:, 6:8, :] = recv[:, 6:8, :]
        places = around(own_cell(), CENTERS[0], boxes, sizes)
        for n in range(len(boxes)):
            chosen[n] = source[places[n]]
        for n in range(len(boxes), chosen.shape[0]):
            chosen[n] = jnp.zeros((8, slots), F32)
        group = LANES // 8
        for g in range(chosen.shape[0] // group):
            cols[:, g * LANES : (g + 1) * LANES] = chosen[g * group : (g + 1) * group].reshape(LANES, slots).T
        one = jnp.ones((1, slots), F32)
        for m, (n, step) in enumerate(images):
            spots = [chosen[n, a : a + 1, :] + (step[a] - 0.5) * length for a in range(3)]
            frames[m] = jnp.concatenate(spots + [one] + spots + [one], axis=0)
        fr, root, part = derived(own[0:3], own[4:5], own[5:6], length)
        wide = [jnp.broadcast_to(row, (tile, slots)) for row in (fr[0:1], fr[1:2], fr[2:3], root, part, own[6:7])]
        acc[...] = jnp.zeros(acc.shape, F32)

        def body(t, carry):
            at = pl.ds(pl.multiple_of(t * tile, tile), tile)
            block = cols[at, :]
            fields = [acc[a] for a in range(3)]
            for n, box in enumerate(boxes):
                row = lambda c: jnp.broadcast_to(block[:, n * 8 + c : n * 8 + c + 1], (tile, slots))
                deltas, ahead = [], []
                for a in range(3):
                    step, nearest = box[a]
                    raw = wide[a] - row(a) if nearest or not step else (wide[a] - step * length) - row(a)
                    if nearest:
                        ahead.append((a, raw > 0.0))
                        raw = raw - jnp.where(ahead[-1][1], length, -length)
                    deltas.append(raw)
                dist_sq = norm(deltas)
                if is_center(box):
                    target = lax.broadcasted_iota(jnp.int32, (tile, slots), 1)
                    keep = target != lax.broadcasted_iota(jnp.int32, (tile, slots), 0) + t * tile
                    dist_sq = jnp.where(keep, dist_sq, 1.0)
                inverse, half_x, tanh, base = terms(wide, dist_sq, row)
                direct = base * tanh
                fields = charge_sum(fields, wide, deltas, direct, row)
                radial = (base * (3.0 * inverse)) * (inverse * (tanh - half_x * (1.0 - tanh)))
                if is_center(box):
                    direct = jnp.where(keep, direct, 0.0)
                    radial = jnp.where(keep, radial, 0.0)
                spot = pl.ds(pl.multiple_of(n * slots + t * tile, tile), tile)
                bhi[spot, :], blo[spot, :] = split(direct)
                for m, (owner, step) in enumerate(images):
                    if owner != n:
                        continue
                    part = radial
                    for a, side in ahead:
                        part = jnp.where(side, part, 0.0) if step[a] > 0 else jnp.where(side, 0.0, part)
                    spot = pl.ds(pl.multiple_of(m * slots + t * tile, tile), tile)
                    ahi[spot, :], alo[spot, :] = split(part)
            for a in range(3):
                acc[a] = fields[a]
            return carry

        lax.fori_loop(0, slots // tile, body, 0)
        rows = [jnp.sum(acc[a], axis=0, keepdims=True) for a in range(3)]
        perm[...] = jnp.concatenate(rows, axis=0)
        send_moments(send, [own[13:14] * row for row in rows], slots)

    return kernel


def build_lhs(lhs, recv, frames, places, images, slots):
    halves = slots // LANES
    upper = lax.broadcasted_iota(jnp.int32, (8, slots), 0) < 4
    known = {}
    for m, (n, _) in enumerate(images):
        if n not in known:
            known[n] = [
                jnp.concatenate(
                    [recv[places[n], a * halves + h : a * halves + h + 1, :] for h in range(halves)], axis=1
                )
                for a in range(3)
            ]
        mu = known[n]
        along = frames[m, 0:1, :] * mu[0] + frames[m, 1:2, :] * mu[1] + frames[m, 2:3, :] * mu[2]
        frame = frames[m]
        whole = lambda row: jnp.broadcast_to(row, (8, slots))
        value = jnp.concatenate(
            [
                frame * jnp.where(upper, whole(mu[0]), whole(mu[1])),
                frame * jnp.where(upper, whole(mu[2]), whole(along)),
            ],
            axis=0,
        )
        lanes = slice(m * slots, (m + 1) * slots)
        for piece in range(3):
            high = value.astype(BF16)
            lhs[piece * 16 : (piece + 1) * 16, lanes] = high
            value = value - high.astype(F32)


def induced_rows(lhs, ahi, alo, bhi, blo, own, perm, count_boxes, slots):
    length = box_length(slots) / CUTOFF
    dot = lambda left, right: jnp.dot(left, right, preferred_element_type=F32)
    near = lhs[:, 0 : count_boxes * slots]
    tensor = dot(lhs[...], ahi[...]) + dot(lhs[...], alo[...])
    plain = dot(near, bhi[...]) + dot(near, blo[...])
    tensor = tensor[0:16] + (tensor[16:32] + tensor[32:48])
    plain = plain[0:16] + (plain[16:32] + plain[32:48])
    spot = [(own[a : a + 1] - 0.5) * length for a in range(3)]
    first = [tensor[4 * a + 3 : 4 * a + 4] for a in range(3)]
    along = spot[0] * first[0] + spot[1] * first[1] + spot[2] * first[2] - tensor[15:16]
    rows = []
    for a in range(3):
        mixed = sum(tensor[4 * b + a : 4 * b + a + 1] * spot[b] for b in range(3))
        value = (spot[a] * along - mixed) + tensor[12 + a : 13 + a]
        rows.append(perm[a : a + 1] + (value - plain[4 * a + 3 : 4 * a + 4]))
    return rows


def induced_kernel(sizes, slots):
    boxes = shell(sizes)
    images = image_list(boxes)

    def kernel(recv, frames, ahi, alo, bhi, blo, own, perm, send, shift, lhs):
        places = around(own_cell(), CENTERS[0], boxes, sizes)
        build_lhs(lhs, recv, frames, places, images, slots)
        rows = induced_rows(lhs, ahi, alo, bhi, blo, own, perm, len(boxes), slots)
        shift[...] = jnp.concatenate([own[14:15] * row for row in rows], axis=0)
        send_moments(send, [own[13:14] * row for row in rows], slots)

    return kernel


def final_kernel(sizes, slots, moves):
    boxes = shell(sizes)
    images = image_list(boxes)
    tile = moves
    halves = slots // LANES
    edge = box_length(slots)
    length = edge / CUTOFF

    def kernel(
        recv, frames, ahi, alo, bhi, blo, own, perm, shift, first_recv, source,
        staying, arrivals, lhs, acc, cols, table, out_stay, out_come, out_sems,
    ):
        cell = own_cell()
        places = around(cell, CENTERS[0], boxes, sizes)
        build_lhs(lhs, recv, frames, places, images, slots)
        field = induced_rows(lhs, ahi, alo, bhi, blo, own, perm, len(boxes), slots)
        remain = own[12:13] > 0.5
        fast = [own[8 + a : 9 + a] + own[15:16] * field[a] for a in range(3)]
        place = [own[a : a + 1] + TIMESTEP * fast[a] / edge for a in range(3)]
        drude = [shift[a : a + 1] for a in range(3)]
        for r, row in enumerate(place + fast + drude):
            out_stay[r] = jnp.where(remain, row, 0.0)
        early = pltpu.make_async_copy(out_stay, staying, out_sems.at[0])
        early.start()

        fill_table(table, cell, boxes, sizes)
        lane = lax.broadcasted_iota(jnp.int32, (1, LANES), 1)
        origin = [linear(cell, [-step for step in unit], sizes) for unit in UNITS]
        extra = jnp.full((8, LANES), -1.0, F32)
        for k in range(6):
            side = (k % 2) * LANES
            row = first_recv[origin[k], 7:8, side : side + LANES]
            row = jnp.broadcast_to(row, (8, LANES))
            fields = [pltpu.roll(row, (k * moves - c * moves) % LANES, 1)[0:1] for c in range(5)]
            block = jnp.concatenate(fields + [extra[0:3]], axis=0)
            extra = jnp.where(lane // moves == k, block, extra)
        slot = extra[0:1]
        slot_col = lax.broadcasted_iota(jnp.int32, (slots, LANES), 0).astype(F32)
        hit = (slot_col == slot).astype(F32)
        got = jnp.zeros((8, LANES), F32)
        moment = jnp.zeros((8, LANES), F32)
        for k in range(6):
            got = jnp.where(lane // moves == k, row_dot(first_recv[origin[k]], hit), got)
            block = recv[origin[k]]
            both = [row_dot(block, hit[h * LANES : (h + 1) * LANES, :]) for h in range(halves)]
            one = [
                sum(both[h][a * halves + h : a * halves + h + 1] for h in range(halves)) for a in range(3)
            ]
            one = jnp.concatenate(one + [jnp.zeros((5, LANES), F32)], axis=0)
            moment = jnp.where(lane // moves == k, one, moment)
        present = slot >= 0.0
        fr, root, part = derived(got[0:3], jnp.where(present, got[4:5], -1.0), got[5:6], length)
        cols[...] = columns(jnp.concatenate([fr, root, part, got[6:7], slot, slot], axis=0))
        acc[...] = jnp.zeros(acc.shape, F32)

        def incoming(k, carry):
            at = pl.ds(pl.multiple_of(k * tile, tile), tile)
            wide, shifted = target_of(cols[at, :], length, 7)
            fields = [jnp.zeros((tile, LANES), F32)] * 3
            for n, box in enumerate(boxes):
                spot = table[(k + 1) * len(boxes) + n]
                for half in range(halves):
                    row = reader(source, spot, half, tile)
                    mu = [
                        jnp.broadcast_to(recv[spot, a * halves + half : a * halves + half + 1, :], (tile, LANES))
                        for a in range(3)
                    ]
                    deltas = offsets(wide, shifted, row, box, length)
                    dist_sq = norm(deltas)
                    if is_center(box):
                        ids = lax.broadcasted_iota(jnp.int32, (tile, LANES), 1) + half * LANES
                        keep = wide[6] != ids.astype(F32)
                        dist_sq = jnp.where(keep, dist_sq, 1.0)
                    inverse, half_x, tanh, base = terms(wide, dist_sq, row)
                    direct = base * tanh
                    radial = (base * (3.0 * inverse)) * (inverse * (tanh - half_x * (1.0 - tanh)))
                    if is_center(box):
                        direct = jnp.where(keep, direct, 0.0)
                        radial = jnp.where(keep, radial, 0.0)
                    pull = jnp.where(wide[5] != row(6), direct, 0.0) * row(3)
                    pull = pull + radial * (deltas[0] * mu[0] + deltas[1] * mu[1] + deltas[2] * mu[2])
                    fields = [fields[a] + (pull * deltas[a] - direct * mu[a]) for a in range(3)]
            for a in range(3):
                acc[a, at, :] = fields[a]
            return carry

        lax.fori_loop(0, 6, incoming, 0)
        pull = rows_of([acc[a] for a in range(3)])
        q = got[3:4]
        qd = got[4:5]
        mass = jnp.where(present, extra[4:5], 1.0)
        gain = KICK * q / mass
        fast = [extra[1 + a : 2 + a] + gain * pull[a] for a in range(3)]
        place = [got[a : a + 1] + TIMESTEP * fast[a] / edge for a in range(3)]
        for k, unit in enumerate(UNITS):
            for a in range(3):
                if unit[a]:
                    place[a] = place[a] - jnp.where(lane // moves == k, float(unit[a]), 0.0)
        safe = jnp.where(present, qd, -1.0) * MOMENT
        drude = [moment[a : a + 1] / safe for a in range(3)]
        record = place + fast + drude + [q, qd, got[5:6], got[6:7], mass]
        for r, row in enumerate(record):
            out_come[r] = jnp.where(present, row, 0.0)[:, 0 : 6 * moves]
        late = pltpu.make_async_copy(out_come, arrivals, out_sems.at[1])
        late.start()
        early.wait()
        late.wait()

    return kernel


def solution(mesh):
    sizes = tuple(mesh.shape[axis] for axis in AXES)
    devices = int(np.prod(sizes))
    boxes = shell(sizes)
    count_boxes = len(boxes)
    count_images = len(image_list(boxes))
    padded_boxes = -(-count_boxes // 16) * 16

    def local(fractions, velocity, charge, drude_charge, screening, labels, masses, counts, leaving):
        slots = charge.shape[-1]
        moves = leaving.shape[-1]
        exchange = lambda block: lax.all_to_all(block, AXES, 0, 0)
        shape = lambda *dims: jax.ShapeDtypeStruct(dims, F32)
        half = lambda *dims: jax.ShapeDtypeStruct(dims, BF16)
        hbm = lambda x: pltpu.with_memory_space_constraint(x, pltpu.HBM)
        moment_shape = (devices, 8, LANES)
        dma = pltpu.SemaphoreType.DMA

        def call(kernel, in_specs, outs, out_specs, scratch, flops, limit):
            return pl.pallas_call(
                kernel,
                in_specs=in_specs,
                out_shape=outs,
                out_specs=out_specs,
                scratch_shapes=scratch,
                compiler_params=pltpu.CompilerParams(vmem_limit_bytes=limit),
                cost_estimate=pl.CostEstimate(flops=flops, bytes_accessed=1 << 20, transcendentals=0),
            )

        flat = [
            fractions.reshape(3, 1, slots),
            velocity.reshape(3, 1, slots),
            charge.reshape(1, slots),
            drude_charge.reshape(1, slots),
            screening.reshape(1, slots),
            labels.reshape(1, slots),
            masses.reshape(1, slots),
            leaving.reshape(6, 1, moves),
        ]
        send, own = call(
            pack_kernel(sizes, slots, moves),
            [smem()] + [anywhere()] * 8,
            (shape(devices, 8, slots), shape(16, slots)),
            (vmem(), vmem()),
            [VMEM(array.shape, array.dtype) for array in flat] + [dma((8,))],
            1 << 20,
            8 << 20,
        )(counts.reshape(1), *[hbm(x) for x in flat])
        first = exchange(send)
        outs = (
            shape(devices, 8, slots),
            shape(count_images, 8, slots),
            half(count_images * slots, slots),
            half(count_images * slots, slots),
            half(count_boxes * slots, slots),
            half(count_boxes * slots, slots),
            shape(3, slots),
            shape(*moment_shape),
        )
        source, frames, ahi, alo, bhi, blo, perm, moments = call(
            field_kernel(sizes, slots, 16),
            [vmem()] * 2,
            outs,
            (vmem(),) * len(outs),
            [
                VMEM((padded_boxes, 8, slots), F32),
                VMEM((slots, padded_boxes * 8), F32),
                VMEM((3, 16, slots), F32),
            ],
            1 << 25,
            8 << 20,
        )(first, own)
        got = exchange(moments)
        tensors = (frames, ahi, alo, bhi, blo, own, perm)
        lhs = VMEM((48, count_images * slots), BF16)
        for _ in range(ITERS - 1):
            moments, shift = call(
                induced_kernel(sizes, slots),
                [vmem()] * 8,
                (shape(*moment_shape), shape(3, slots)),
                (vmem(),) * 2,
                [lhs],
                1 << 24,
                4 << 20,
            )(got, *tensors)
            got = exchange(moments)
        staying, arrivals = call(
            final_kernel(sizes, slots, moves),
            [vmem()] * 11,
            (pltpu.HBM((9, 1, slots), F32), pltpu.HBM((14, 1, 6 * moves), F32)),
            (anywhere(), anywhere()),
            [
                lhs,
                VMEM((3, LANES, LANES), F32),
                VMEM((LANES, LANES), F32),
                pltpu.SMEM((len(CENTERS) * count_boxes,), jnp.int32),
                VMEM((9, 1, slots), F32),
                VMEM((14, 1, 6 * moves), F32),
                dma((2,)),
            ],
            1 << 24,
            8 << 20,
        )(got, *tensors, shift, first, source)
        return staying.reshape(1, 1, 1, 9, slots), arrivals.reshape(1, 1, 1, 14, 6 * moves)

    box = P("gx", "gy", "gz", None)
    rows = P("gx", "gy", "gz", None, None)
    return jax.shard_map(
        local,
        mesh=mesh,
        in_specs=(rows, rows, box, box, box, box, box, P("gx", "gy", "gz"), rows),
        out_specs=(rows, rows),
        check_vma=False,
    )
```

time: 86.1 us -> 72.6 us (0.84)
  Pallas kernels: 41.1 us -> 23.4 us
  blocking collectives: 40.9 us -> 47.6 us
  starting transfers between devices: 2.55 us -> 0 us
    pallas_call x5 -> x4, Pallas kernels: 39.6 us -> 21.9 us  [the longest x1 10.6 us: local(): call(field_kernel(sizes, slots, 16), [vmem()] * 2, outs, (vmem(),) * len(...]
    all_to_all x3 -> x4, blocking collectives: 40.9 us -> 47.6 us  [local(): exchange = lambda block: lax.all_to_all(block, AXES, 0, 0)]
    all_to_all x1 -> x0, starting transfers between devices: 2.55 us -> none  [local(): exchange = lambda block: lax.all_to_all(block, AXES, 0, 0)]
  transfers between devices with their start and end apart: 1 -> 0, of which waited for: 0 -> 0; matrix products, arithmetic and copies ran while one was open for 0% -> 0% of each run, Pallas kernels for 13% -> 0%
where the time goes in v1:
time: 72.6 us; the launch traced here: 72.4 us
  blocking collectives  47.6 us (66%)
  Pallas kernels  23.4 us (32%)
  between operations  1.3 us (2%)
    all_to_all x4, blocking collectives, local(): exchange = lambda block: lax.all_to_all(block, AXES, 0, 0)  47.6 us
    pallas_call x1, Pallas kernels, local(): call(field_kernel(sizes, slots, 16), [vmem()] * 2, outs, (vmem(),) * len(...  10.6 us
    pallas_call x1, Pallas kernels, local(): call(final_kernel(sizes, slots, moves), [vmem()] * 11, (pltpu.HBM((9, 1,...  7.19 us
    pallas_call x2, Pallas kernels, local(): call(induced_kernel(sizes, slots), [vmem()] * 8, (shape(*moment_shape), s...  4.07 us
    pallas_call x1, Pallas kernels, local(): call(pack_kernel(sizes, slots, moves), [smem()] + [anywhere()] * 8, (shap...  1.56 us

profile of v1, /device:TPU:0, one launch (start us, length us, event | category | flops | bytes accessed | tf_op | source)
XLA Modules:
  0.0 72.4 jit_solution(2668135679747112100)
XLA Ops:
  1.3 1.6 %shard_map.104 = (f32[32,8,256]{2,1,0:T(8,128)S(1)}, f32[16,256]{1,0:T(8,128)S(1)}) custom-call(s32[1]{0:T(128)} %bitcast.15.refs_0_, f32[3,1,256]{2,1,0:T(1,128)} %bitcast.16, f32[3,1,256]{2,1,0:T(1,128)} %bitcast.17, f32[1,256]{1,0:T(1,128)} %bitcast.19, f32[1,256]{1,0:T(1,128)} %bitcast.20, f32[1,256]{1,0:T(1,128)} %bitcast.21, s32[1,256]{1,0:T(1,128)} %bitcast.22, ...), custom_call_target="tpu_custom_call" | custom-call | flops 1048576 | bytes 1048576 | tf_op jit(solution)/shard_map/pallas_call | solution.py:509
  2.8 17.6 %all_to_all.20.recv.first_recv = f32[32,8,256]{2,1,0:T(8,128)S(1)} all-to-all(f32[32,8,256]{2,1,0:T(8,128)S(1)} %get-tuple-element.17), channel_id=1, replica_groups=mesh['gx'=4,'gy'=4,'gz'=2] {'gx','gy','gz'}, dimensions={0} | all-to-all | bytes 524288 | tf_op jit(solution)/shard_map/all_to_all | solution.py:481
  20.4 10.6 %shard_map.105 = (f32[32,8,256]{2,1,0:T(8,128)S(1)}, f32[27,8,256]{2,1,0:T(8,128)S(1)}, bf16[6912,256]{1,0:T(8,128)(2,1)S(1)}, bf16[6912,256]{1,0:T(8,128)(2,1)S...) custom-call(f32[32,8,256]{2,1,0:T(8,128)S(1)} %all_to_all.20.recv.fi, ...), custom_call_target="tpu_custom_call" | custom-call | flops 33554432 | bytes 1048576 | tf_op jit(solution)/shard_map/pallas_call | solution.py:529
  31.0 10.1 %all_to_all.21.recv = f32[32,8,128]{2,1,0:T(8,128)S(1)} all-to-all(f32[32,8,128]{2,1,0:T(8,128)S(1)} %get-tuple-element.19), channel_id=1, replica_groups=mesh['gx'=4,'gy'=4,'gz'=2] {'gx','gy','gz'}, dimensions={0} | all-to-all | bytes 262144 | tf_op jit(solution)/shard_map/all_to_all | solution.py:481
  41.2 2.3 %shard_map.106 = (f32[32,8,128]{2,1,0:T(8,128)S(1)}, f32[3,256]{1,0:T(4,128)}) custom-call(f32[32,8,128]{2,1,0:T(8,128)S(1)} %all_to_all.21.recv, f32[27,8,256]{2,1,0:T(8,128)S(1)} %get-tuple-element.20.frames, bf16[6912,256]{1,0:T(8,128)(2,1)S(1)} %get-tuple-element.21.ahi, bf16[6912,256]{1,0:T(8,128)(2,1)S(1)} %get-tuple-element.22.alo, ...), custom_call_target="tpu_custom_call" | custom-call | flops 16777216 | bytes 1048576 | tf_op jit(solution)/shard_map/pallas_call | solution.py:546
  43.5 10.0 %all_to_all.22.recv = f32[32,8,128]{2,1,0:T(8,128)S(1)} all-to-all(f32[32,8,128]{2,1,0:T(8,128)S(1)} %get-tuple-element.26), channel_id=1, replica_groups=mesh['gx'=4,'gy'=4,'gz'=2] {'gx','gy','gz'}, dimensions={0} | all-to-all | bytes 262144 | tf_op jit(solution)/shard_map/all_to_all | solution.py:481
  53.5 1.7 %shard_map.107 = (f32[32,8,128]{2,1,0:T(8,128)S(1)}, f32[3,256]{1,0:T(4,128)S(1)}) custom-call(f32[32,8,128]{2,1,0:T(8,128)S(1)} %all_to_all.22.recv, f32[27,8,256]{2,1,0:T(8,128)S(1)} %get-tuple-element.20.frames, bf16[6912,256]{1,0:T(8,128)(2,1)S(1)} %get-tuple-element.21.ahi, bf16[6912,256]{1,0:T(8,128)(2,1)S(1)} %get-tuple-element.22.alo, ...), custom_call_target="tpu_custom_call" | custom-call | flops 16777216 | bytes 1048576 | tf_op jit(solution)/shard_map/pallas_call | solution.py:546
  55.2 10.0 %all_to_all.23.recv = f32[32,8,128]{2,1,0:T(8,128)S(1)} all-to-all(f32[32,8,128]{2,1,0:T(8,128)S(1)} %get-tuple-element.27), channel_id=1, replica_groups=mesh['gx'=4,'gy'=4,'gz'=2] {'gx','gy','gz'}, dimensions={0} | all-to-all | bytes 262144 | tf_op jit(solution)/shard_map/all_to_all | solution.py:481
  65.2 7.2 %shard_map.108 = (f32[9,1,256]{2,1,0:T(1,128)}, f32[14,1,96]{2,1,0:T(1,128)}) custom-call(f32[32,8,128]{2,1,0:T(8,128)S(1)} %all_to_all.23.recv, f32[27,8,256]{2,1,0:T(8,128)S(1)} %get-tuple-element.20.frames, bf16[6912,256]{1,0:T(8,128)(2,1)S(1)} %get-tuple-element.21.ahi, bf16[6912,256]{1,0:T(8,128)(2,1)S(1)} %get-tuple-element.22.alo, ...), custom_call_target="tpu_custom_call" | custom-call | flops 16777216 | bytes 1048576 | tf_op jit(solution)/shard_map/pallas_call | solution.py:556

commit v2 on v1

--- a/solution.py
+++ b/solution.py
@@ -20,7 +20,6 @@
 MOMENT = 2.0 / CUTOFF**3
 F32 = jnp.float32
 BF16 = jnp.bfloat16
-HIGHEST = lax.Precision.HIGHEST
 VMEM = pltpu.VMEM
 
 
@@ -69,8 +68,20 @@
             table[g * len(boxes) + n] = place
 
 
-def row_dot(rows, hit):
-    return jnp.dot(rows, hit, precision=HIGHEST, preferred_element_type=F32)
+def pieces_of(values):
+    pieces = []
+    for _ in range(3):
+        piece = values.astype(BF16).astype(F32)
+        pieces.append(piece)
+        values = values - piece
+    return pieces
+
+
+def pick(blocks, hit):
+    count = blocks.shape[0]
+    stacked = jnp.concatenate(pieces_of(blocks), axis=0).astype(BF16)
+    got = jnp.dot(stacked, hit, preferred_element_type=F32)
+    return (got[0:count] + got[count : 2 * count]) + got[2 * count :]
 
 
 def pack_kernel(sizes, slots, moves):
@@ -100,29 +111,26 @@
             lax.broadcasted_iota(jnp.int32, (moves, LANES), 1) % moves
             == lax.broadcasted_iota(jnp.int32, (moves, LANES), 0)
         ).astype(F32)
-        repeated = row_dot(lv, spread)
+        repeated = jnp.dot(lv.astype(BF16), spread.astype(BF16), preferred_element_type=F32)
         slot_col = lax.broadcasted_iota(jnp.int32, (slots, LANES), 0).astype(F32)
         values = jnp.concatenate([ve, ms, jnp.zeros((4, slots), F32)], axis=0)
         field = lax.broadcasted_iota(jnp.int32, (8, LANES), 1) // moves - 1
         wanted = field == lax.broadcasted_iota(jnp.int32, (8, LANES), 0)
         first = lax.broadcasted_iota(jnp.int32, (1, LANES), 1) < moves
-        departed = jnp.zeros((1, slots), F32)
         statics = jnp.concatenate([fr, q, qd, sc, lb, jnp.zeros((1, slots), F32)], axis=0)
         send[...] = jnp.broadcast_to(statics[None], (devices, 8, slots))
-        ones = jnp.ones((8, LANES), BF16)
+        hits = jnp.concatenate(
+            [(slot_col == repeated[k : k + 1]).astype(F32).astype(BF16) for k in range(6)], axis=1
+        )
+        picked = pick(values, hits)
         for k, unit in enumerate(UNITS):
-            hit = slot_col == repeated[k : k + 1]
-            picked = row_dot(values, hit.astype(F32))
-            row = jnp.sum(jnp.where(wanted, picked, 0.0), axis=0, keepdims=True)
+            mine = picked[:, k * LANES : (k + 1) * LANES]
+            row = jnp.sum(jnp.where(wanted, mine, 0.0), axis=0, keepdims=True)
             row = jnp.where(first, repeated[k : k + 1], row)
             side = (k % 2) * LANES
             send[linear(cell, unit, sizes), 7:8, side : side + LANES] = row
-            departed = departed + lax.dot_general(
-                ones,
-                hit.astype(F32).astype(BF16),
-                (((1,), (1,)), ((), ())),
-                preferred_element_type=F32,
-            )[0:1]
+        ones = jnp.ones((16, 6 * LANES), BF16)
+        departed = lax.dot_general(ones, hits, (((1,), (1,)), ((), ())), preferred_element_type=F32)[0:1]
         alive = live.astype(F32)
         gain = jnp.where(live, DRUDE_GAIN * qd, 0.0)
         own[...] = jnp.concatenate(
@@ -178,8 +186,8 @@
     fade = inverse * jnp.maximum(1.0 - dist_sq, 0.0)
     half_x = (wide[3] * row(5) + wide[4] * row(4)) * (dist_sq * (dist_sq * inverse))
     tanh = jnp.tanh(half_x)
-    root = lax.rsqrt(1.0 + tanh)
-    base = ((fade * fade) * inverse) * (root * root)
+    root = fade * lax.rsqrt(1.0 + tanh)
+    base = (root * root) * inverse
     return inverse, half_x, tanh, base
 
 
@@ -206,10 +214,11 @@
 
 
 def send_moments(send, moments, slots):
-    rows = [m[:, h * LANES : (h + 1) * LANES] for m in moments for h in range(slots // LANES)]
-    rows.append(jnp.zeros((send.shape[1] - len(rows), LANES), F32))
-    block = jnp.concatenate(rows, axis=0)
-    send[...] = jnp.broadcast_to(block[None], send.shape)
+    halves = slots // LANES
+    for a in range(3):
+        for h in range(halves):
+            row = moments[a][:, h * LANES : (h + 1) * LANES]
+            send[:, a * halves + h] = jnp.broadcast_to(row[None], (send.shape[0], 1, LANES))
 
 
 def split(values):
@@ -267,7 +276,7 @@
                 inverse, half_x, tanh, base = terms(wide, dist_sq, row)
                 direct = base * tanh
                 fields = charge_sum(fields, wide, deltas, direct, row)
-                radial = (base * (3.0 * inverse)) * (inverse * (tanh - half_x * (1.0 - tanh)))
+                radial = base * (inverse * inverse) * (tanh - half_x * (1.0 - tanh))
                 if is_center(box):
                     direct = jnp.where(keep, direct, 0.0)
                     radial = jnp.where(keep, radial, 0.0)
@@ -301,7 +310,7 @@
         if n not in known:
             known[n] = [
                 jnp.concatenate(
-                    [recv[places[n], a * halves + h : a * halves + h + 1, :] for h in range(halves)], axis=1
+                    [recv[places[n], a * halves + h] for h in range(halves)], axis=1
                 )
                 for a in range(3)
             ]
@@ -323,13 +332,15 @@
             value = value - high.astype(F32)
 
 
-def induced_rows(lhs, ahi, alo, bhi, blo, own, perm, count_boxes, slots):
+def product(lhs, high, low, at):
+    left = lhs[:, at]
+    dot = lambda right: jnp.dot(left, right[at, :], preferred_element_type=F32)
+    return dot(high) + dot(low)
+
+
+def induced_rows(tensor, plain, own, perm, slots):
     length = box_length(slots) / CUTOFF
-    dot = lambda left, right: jnp.dot(left, right, preferred_element_type=F32)
-    near = lhs[:, 0 : count_boxes * slots]
-    tensor = dot(lhs[...], ahi[...]) + dot(lhs[...], alo[...])
-    plain = dot(near, bhi[...]) + dot(near, blo[...])
-    tensor = tensor[0:16] + (tensor[16:32] + tensor[32:48])
+    tensor = 3.0 * (tensor[0:16] + (tensor[16:32] + tensor[32:48]))
     plain = plain[0:16] + (plain[16:32] + plain[32:48])
     spot = [(own[a : a + 1] - 0.5) * length for a in range(3)]
     first = [tensor[4 * a + 3 : 4 * a + 4] for a in range(3)]
@@ -349,7 +360,9 @@
     def kernel(recv, frames, ahi, alo, bhi, blo, own, perm, send, shift, lhs):
         places = around(own_cell(), CENTERS[0], boxes, sizes)
         build_lhs(lhs, recv, frames, places, images, slots)
-        rows = induced_rows(lhs, ahi, alo, bhi, blo, own, perm, len(boxes), slots)
+        tensor = product(lhs, ahi, alo, slice(0, len(images) * slots))
+        plain = product(lhs, bhi, blo, slice(0, len(boxes) * slots))
+        rows = induced_rows(tensor, plain, own, perm, slots)
         shift[...] = jnp.concatenate([own[14:15] * row for row in rows], axis=0)
         send_moments(send, [own[13:14] * row for row in rows], slots)
 
@@ -366,21 +379,11 @@
 
     def kernel(
         recv, frames, ahi, alo, bhi, blo, own, perm, shift, first_recv, source,
-        staying, arrivals, lhs, acc, cols, table, out_stay, out_come, out_sems,
+        staying, arrivals, lhs, sums, acc, targets, table, out_stay, out_come, out_sems,
     ):
         cell = own_cell()
         places = around(cell, CENTERS[0], boxes, sizes)
         build_lhs(lhs, recv, frames, places, images, slots)
-        field = induced_rows(lhs, ahi, alo, bhi, blo, own, perm, len(boxes), slots)
-        remain = own[12:13] > 0.5
-        fast = [own[8 + a : 9 + a] + own[15:16] * field[a] for a in range(3)]
-        place = [own[a : a + 1] + TIMESTEP * fast[a] / edge for a in range(3)]
-        drude = [shift[a : a + 1] for a in range(3)]
-        for r, row in enumerate(place + fast + drude):
-            out_stay[r] = jnp.where(remain, row, 0.0)
-        early = pltpu.make_async_copy(out_stay, staying, out_sems.at[0])
-        early.start()
-
         fill_table(table, cell, boxes, sizes)
         lane = lax.broadcasted_iota(jnp.int32, (1, LANES), 1)
         origin = [linear(cell, [-step for step in unit], sizes) for unit in UNITS]
@@ -394,33 +397,49 @@
             extra = jnp.where(lane // moves == k, block, extra)
         slot = extra[0:1]
         slot_col = lax.broadcasted_iota(jnp.int32, (slots, LANES), 0).astype(F32)
-        hit = (slot_col == slot).astype(F32)
+        hit = (slot_col == slot).astype(F32).astype(BF16)
+        blank = jnp.zeros((5, slots), F32)
+        blocks = []
+        for k in range(6):
+            blocks.append(first_recv[origin[k]])
+            for a in range(3):
+                blocks.append(
+                    jnp.concatenate([recv[origin[k], a * halves + h] for h in range(halves)], axis=1)
+                )
+            blocks.append(blank)
+        taken = pick(jnp.concatenate(blocks, axis=0), hit)
         got = jnp.zeros((8, LANES), F32)
         moment = jnp.zeros((8, LANES), F32)
         for k in range(6):
-            got = jnp.where(lane // moves == k, row_dot(first_recv[origin[k]], hit), got)
-            block = recv[origin[k]]
-            both = [row_dot(block, hit[h * LANES : (h + 1) * LANES, :]) for h in range(halves)]
-            one = [
-                sum(both[h][a * halves + h : a * halves + h + 1] for h in range(halves)) for a in range(3)
-            ]
-            one = jnp.concatenate(one + [jnp.zeros((5, LANES), F32)], axis=0)
-            moment = jnp.where(lane // moves == k, one, moment)
+            got = jnp.where(lane // moves == k, taken[16 * k : 16 * k + 8], got)
+            moment = jnp.where(lane // moves == k, taken[16 * k + 8 : 16 * k + 16], moment)
         present = slot >= 0.0
         fr, root, part = derived(got[0:3], jnp.where(present, got[4:5], -1.0), got[5:6], length)
-        cols[...] = columns(jnp.concatenate([fr, root, part, got[6:7], slot, slot], axis=0))
+        cols = columns(jnp.concatenate([fr, root, part, got[6:7], slot, slot], axis=0))
+        for k in range(6):
+            for c, value in enumerate(target_of(cols[k * tile : (k + 1) * tile], length, 7)[0]):
+                targets[k, c] = value
         acc[...] = jnp.zeros(acc.shape, F32)
+        steps = [len(images) // 6 * slots, len(boxes) // 6 * slots]
+        for which, (high, low, count) in enumerate(((ahi, alo, len(images)), (bhi, blo, len(boxes)))):
+            sums[which] = jnp.zeros((48, slots), F32)
+            if count * slots > 6 * steps[which]:
+                sums[which] = product(lhs, high, low, slice(6 * steps[which], count * slots))
 
         def incoming(k, carry):
+            for which, (high, low) in enumerate(((ahi, alo), (bhi, blo))):
+                part = pl.ds(pl.multiple_of(k * steps[which], LANES), steps[which])
+                sums[which] = sums[which] + product(lhs, high, low, part)
             at = pl.ds(pl.multiple_of(k * tile, tile), tile)
-            wide, shifted = target_of(cols[at, :], length, 7)
+            wide = [targets[k, c] for c in range(7)]
+            shifted = [{-1: wide[a] + length, 0: wide[a], 1: wide[a] - length} for a in range(3)]
             fields = [jnp.zeros((tile, LANES), F32)] * 3
             for n, box in enumerate(boxes):
                 spot = table[(k + 1) * len(boxes) + n]
                 for half in range(halves):
                     row = reader(source, spot, half, tile)
                     mu = [
-                        jnp.broadcast_to(recv[spot, a * halves + half : a * halves + half + 1, :], (tile, LANES))
+                        jnp.broadcast_to(recv[spot, a * halves + half], (tile, LANES))
                         for a in range(3)
                     ]
                     deltas = offsets(wide, shifted, row, box, length)
@@ -431,18 +450,28 @@
                         dist_sq = jnp.where(keep, dist_sq, 1.0)
                     inverse, half_x, tanh, base = terms(wide, dist_sq, row)
                     direct = base * tanh
-                    radial = (base * (3.0 * inverse)) * (inverse * (tanh - half_x * (1.0 - tanh)))
+                    radial = base * (inverse * inverse) * (tanh - half_x * (1.0 - tanh))
                     if is_center(box):
                         direct = jnp.where(keep, direct, 0.0)
                         radial = jnp.where(keep, radial, 0.0)
                     pull = jnp.where(wide[5] != row(6), direct, 0.0) * row(3)
-                    pull = pull + radial * (deltas[0] * mu[0] + deltas[1] * mu[1] + deltas[2] * mu[2])
+                    pull = pull + (3.0 * radial) * (deltas[0] * mu[0] + deltas[1] * mu[1] + deltas[2] * mu[2])
                     fields = [fields[a] + (pull * deltas[a] - direct * mu[a]) for a in range(3)]
             for a in range(3):
                 acc[a, at, :] = fields[a]
             return carry
 
         lax.fori_loop(0, 6, incoming, 0)
+        field = induced_rows(sums[0], sums[1], own, perm, slots)
+        remain = own[12:13] > 0.5
+        fast = [own[8 + a : 9 + a] + own[15:16] * field[a] for a in range(3)]
+        place = [own[a : a + 1] + TIMESTEP * fast[a] / edge for a in range(3)]
+        drude = [shift[a : a + 1] for a in range(3)]
+        for r, row in enumerate(place + fast + drude):
+            out_stay[r] = jnp.where(remain, row, 0.0)
+        early = pltpu.make_async_copy(out_stay, staying, out_sems.at[0])
+        early.start()
+
         pull = rows_of([acc[a] for a in range(3)])
         q = got[3:4]
         qd = got[4:5]
@@ -482,7 +511,7 @@
         shape = lambda *dims: jax.ShapeDtypeStruct(dims, F32)
         half = lambda *dims: jax.ShapeDtypeStruct(dims, BF16)
         hbm = lambda x: pltpu.with_memory_space_constraint(x, pltpu.HBM)
-        moment_shape = (devices, 8, LANES)
+        moment_shape = (devices, 3 * (slots // LANES), 1, LANES)
         dma = pltpu.SemaphoreType.DMA
 
         def call(kernel, in_specs, outs, out_specs, scratch, flops, limit):
@@ -527,14 +556,14 @@
             shape(*moment_shape),
         )
         source, frames, ahi, alo, bhi, blo, perm, moments = call(
-            field_kernel(sizes, slots, 16),
+            field_kernel(sizes, slots, 32),
             [vmem()] * 2,
             outs,
             (vmem(),) * len(outs),
             [
                 VMEM((padded_boxes, 8, slots), F32),
                 VMEM((slots, padded_boxes * 8), F32),
-                VMEM((3, 16, slots), F32),
+                VMEM((3, 32, slots), F32),
             ],
             1 << 25,
             8 << 20,
@@ -560,8 +589,9 @@
             (anywhere(), anywhere()),
             [
                 lhs,
+                VMEM((2, 48, slots), F32),
                 VMEM((3, LANES, LANES), F32),
-                VMEM((LANES, LANES), F32),
+                VMEM((6, 7, moves, LANES), F32),
                 pltpu.SMEM((len(CENTERS) * count_boxes,), jnp.int32),
                 VMEM((9, 1, slots), F32),
                 VMEM((14, 1, 6 * moves), F32),

time: 72.6 us -> 68.7 us (0.946)
  Pallas kernels: 23.4 us -> 21.1 us
  blocking collectives: 47.6 us -> 46.1 us
    pallas_call x1, Pallas kernels: 7.19 us -> 5.45 us  [local(): call(final_kernel(sizes, slots, moves), [vmem()] * 11, (pltpu.HBM((9, 1,...]
    all_to_all x4, blocking collectives: 47.6 us -> 46.1 us  [local(): exchange = lambda block: lax.all_to_all(block, AXES, 0, 0)]
where the time goes in v2:
time: 68.7 us; the launch traced here: 68.4 us
  blocking collectives  46.1 us (67%)
  Pallas kernels  21.1 us (31%)
  between operations  1.3 us (2%)
    all_to_all x4, blocking collectives, local(): exchange = lambda block: lax.all_to_all(block, AXES, 0, 0)  46.1 us
    pallas_call x1, Pallas kernels, local(): call(field_kernel(sizes, slots, 32), [vmem()] * 2, outs, (vmem(),) * len(...  10.2 us
    pallas_call x1, Pallas kernels, local(): call(final_kernel(sizes, slots, moves), [vmem()] * 11, (pltpu.HBM((9, 1,...  5.45 us
    pallas_call x2, Pallas kernels, local(): call(induced_kernel(sizes, slots), [vmem()] * 8, (shape(*moment_shape), s...  4.16 us

profile of v2, /device:TPU:0, one launch (start us, length us, event | category | flops | bytes accessed | tf_op | source)
XLA Modules:
  0.0 68.4 jit_solution(1604584286307515688)
XLA Ops:
  1.3 1.3 %shard_map.104 = (f32[32,8,256]{2,1,0:T(8,128)S(1)}, f32[16,256]{1,0:T(8,128)S(1)}) custom-call(s32[1]{0:T(128)} %bitcast.15.refs_0_, f32[3,1,256]{2,1,0:T(1,128)} %bitcast.16, f32[3,1,256]{2,1,0:T(1,128)} %bitcast.17, f32[1,256]{1,0:T(1,128)} %bitcast.19, f32[1,256]{1,0:T(1,128)} %bitcast.20, f32[1,256]{1,0:T(1,128)} %bitcast.21, s32[1,256]{1,0:T(1,128)} %bitcast.22, ...), custom_call_target="tpu_custom_call" | custom-call | flops 1048576 | bytes 1048576 | tf_op jit(solution)/shard_map/pallas_call | solution.py:538
  2.6 17.6 %all_to_all.20.recv.first_recv = f32[32,8,256]{2,1,0:T(8,128)S(1)} all-to-all(f32[32,8,256]{2,1,0:T(8,128)S(1)} %get-tuple-element.17), channel_id=1, replica_groups=mesh['gx'=4,'gy'=4,'gz'=2] {'gx','gy','gz'}, dimensions={0} | all-to-all | bytes 524288 | tf_op jit(solution)/shard_map/all_to_all | solution.py:510
  20.2 10.2 %shard_map.105 = (f32[32,8,256]{2,1,0:T(8,128)S(1)}, f32[27,8,256]{2,1,0:T(8,128)S(1)}, bf16[6912,256]{1,0:T(8,128)(2,1)S(1)}, bf16[6912,256]{1,0:T(8,128)(2,1)S...) custom-call(f32[32,8,256]{2,1,0:T(8,128)S(1)} %all_to_all.20.recv.fi, ...), custom_call_target="tpu_custom_call" | custom-call | flops 33554432 | bytes 1048576 | tf_op jit(solution)/shard_map/pallas_call | solution.py:558
  30.3 9.9 %all_to_all.21.recv = f32[32,6,1,128]{3,2,1,0:T(1,128)S(1)} all-to-all(f32[32,6,1,128]{3,2,1,0:T(1,128)S(1)} %get-tuple-element.19), channel_id=1, replica_groups=mesh['gx'=4,'gy'=4,'gz'=2] {'gx','gy','gz'}, dimensions={0} | all-to-all | bytes 196608 | tf_op jit(solution)/shard_map/all_to_all | solution.py:510
  40.3 2.4 %shard_map.106 = (f32[32,6,1,128]{3,2,1,0:T(1,128)S(1)}, f32[3,256]{1,0:T(4,128)}) custom-call(f32[32,6,1,128]{3,2,1,0:T(1,128)S(1)} %all_to_all.21.recv, f32[27,8,256]{2,1,0:T(8,128)S(1)} %get-tuple-element.20.frames, bf16[6912,256]{1,0:T(8,128)(2,1)S(1)} %get-tuple-element.21.ahi, bf16[6912,256]{1,0:T(8,128)(2,1)S(1)} %get-tuple-element.22.alo, ...), custom_call_target="tpu_custom_call" | custom-call | flops 16777216 | bytes 1048576 | tf_op jit(solution)/shard_map/pallas_call | solution.py:575
  42.7 9.3 %all_to_all.22.recv = f32[32,6,1,128]{3,2,1,0:T(1,128)S(1)} all-to-all(f32[32,6,1,128]{3,2,1,0:T(1,128)S(1)} %get-tuple-element.26), channel_id=1, replica_groups=mesh['gx'=4,'gy'=4,'gz'=2] {'gx','gy','gz'}, dimensions={0} | all-to-all | bytes 196608 | tf_op jit(solution)/shard_map/all_to_all | solution.py:510
  51.9 1.8 %shard_map.107 = (f32[32,6,1,128]{3,2,1,0:T(1,128)S(1)}, f32[3,256]{1,0:T(4,128)S(1)}) custom-call(f32[32,6,1,128]{3,2,1,0:T(1,128)S(1)} %all_to_all.22.recv, f32[27,8,256]{2,1,0:T(8,128)S(1)} %get-tuple-element.20.frames, bf16[6912,256]{1,0:T(8,128)(2,1)S(1)} %get-tuple-element.21.ahi, bf16[6912,256]{1,0:T(8,128)(2,1)S(1)} %get-tuple-element.22.alo, ...), custom_call_target="tpu_custom_call" | custom-call | flops 16777216 | bytes 1048576 | tf_op jit(solution)/shard_map/pallas_call | solution.py:575
  53.7 9.3 %all_to_all.23.recv = f32[32,6,1,128]{3,2,1,0:T(1,128)S(1)} all-to-all(f32[32,6,1,128]{3,2,1,0:T(1,128)S(1)} %get-tuple-element.27), channel_id=1, replica_groups=mesh['gx'=4,'gy'=4,'gz'=2] {'gx','gy','gz'}, dimensions={0} | all-to-all | bytes 196608 | tf_op jit(solution)/shard_map/all_to_all | solution.py:510
  63.0 5.4 %shard_map.108 = (f32[9,1,256]{2,1,0:T(1,128)}, f32[14,1,96]{2,1,0:T(1,128)}) custom-call(f32[32,6,1,128]{3,2,1,0:T(1,128)S(1)} %all_to_all.23.recv, f32[27,8,256]{2,1,0:T(8,128)S(1)} %get-tuple-element.20.frames, bf16[6912,256]{1,0:T(8,128)(2,1)S(1)} %get-tuple-element.21.ahi, bf16[6912,256]{1,0:T(8,128)(2,1)S(1)} %get-tuple-element.22.alo, ...), custom_call_target="tpu_custom_call" | custom-call | flops 16777216 | bytes 1048576 | tf_op jit(solution)/shard_map/pallas_call | solution.py:585

commit v3 on v2

--- a/solution.py
+++ b/solution.py
@@ -221,9 +221,9 @@
             send[:, a * halves + h] = jnp.broadcast_to(row[None], (send.shape[0], 1, LANES))
 
 
-def split(values):
-    high = values.astype(BF16)
-    return high, (values - high.astype(F32)).astype(BF16)
+def split(values, high, low, spot):
+    high[spot, :] = values.astype(BF16)
+    low[spot, :] = (values - high[spot, :].astype(F32)).astype(BF16)
 
 
 def field_kernel(sizes, slots, tile):
@@ -231,7 +231,7 @@
     images = image_list(boxes)
     length = box_length(slots) / CUTOFF
 
-    def kernel(recv, own, source, frames, ahi, alo, bhi, blo, perm, send, chosen, cols, acc):
+    def kernel(recv, own, source, frames, ahi, alo, bhi, blo, perm, send, chosen, cols, acc, ready):
         fr, root, part = derived(recv[:, 0:3, :], recv[:, 4:5, :], recv[:, 5:6, :], length)
         source[:, 0:3, :] = fr
         source[:, 3:4, :] = (2.0 / CUTOFF**2) * recv[:, 3:4, :]
@@ -257,9 +257,14 @@
         def body(t, carry):
             at = pl.ds(pl.multiple_of(t * tile, tile), tile)
             block = cols[at, :]
+            after = pl.ds(pl.multiple_of(jnp.minimum(t + 1, slots // tile - 1) * tile, tile), tile)
+            upcoming = cols[after, :]
             fields = [acc[a] for a in range(3)]
             for n, box in enumerate(boxes):
-                row = lambda c: jnp.broadcast_to(block[:, n * 8 + c : n * 8 + c + 1], (tile, slots))
+                if n == 0:
+                    row = lambda c: jnp.concatenate([ready[c]] * (slots // LANES), axis=1)
+                else:
+                    row = lambda c: jnp.broadcast_to(block[:, n * 8 + c : n * 8 + c + 1], (tile, slots))
                 deltas, ahead = [], []
                 for a in range(3):
                     step, nearest = box[a]
@@ -275,13 +280,17 @@
                     dist_sq = jnp.where(keep, dist_sq, 1.0)
                 inverse, half_x, tanh, base = terms(wide, dist_sq, row)
                 direct = base * tanh
-                fields = charge_sum(fields, wide, deltas, direct, row)
+                weight = jnp.where(wide[5] != row(6), direct, 0.0) * row(3)
+                fields = [
+                    fields[a] + jnp.sum((weight * deltas[a]).reshape(tile // 8, 8, slots), axis=0)
+                    for a in range(3)
+                ]
                 radial = base * (inverse * inverse) * (tanh - half_x * (1.0 - tanh))
                 if is_center(box):
                     direct = jnp.where(keep, direct, 0.0)
                     radial = jnp.where(keep, radial, 0.0)
                 spot = pl.ds(pl.multiple_of(n * slots + t * tile, tile), tile)
-                bhi[spot, :], blo[spot, :] = split(direct)
+                split(direct, bhi, blo, spot)
                 for m, (owner, step) in enumerate(images):
                     if owner != n:
                         continue
@@ -289,10 +298,15 @@
                     for a, side in ahead:
                         part = jnp.where(side, part, 0.0) if step[a] > 0 else jnp.where(side, 0.0, part)
                     spot = pl.ds(pl.multiple_of(m * slots + t * tile, tile), tile)
-                    ahi[spot, :], alo[spot, :] = split(part)
+                    split(part, ahi, alo, spot)
             for a in range(3):
                 acc[a] = fields[a]
+            for c in range(7):
+                ready[c] = jnp.broadcast_to(upcoming[:, c : c + 1], (tile, LANES))
             return carry
+
+        for c in range(7):
+            ready[c] = jnp.broadcast_to(cols[0:tile, c : c + 1], (tile, LANES))
 
         lax.fori_loop(0, slots // tile, body, 0)
         rows = [jnp.sum(acc[a], axis=0, keepdims=True) for a in range(3)]
@@ -353,18 +367,56 @@
     return rows
 
 
-def induced_kernel(sizes, slots):
+def arrival_records(first_recv, origin, moves, slots):
+    lane = lax.broadcasted_iota(jnp.int32, (1, LANES), 1)
+    extra = jnp.full((8, LANES), -1.0, F32)
+    for k in range(6):
+        side = (k % 2) * LANES
+        row = first_recv[origin[k], 7:8, side : side + LANES]
+        row = jnp.broadcast_to(row, (8, LANES))
+        fields = [pltpu.roll(row, (k * moves - c * moves) % LANES, 1)[0:1] for c in range(5)]
+        block = jnp.concatenate(fields + [extra[0:3]], axis=0)
+        extra = jnp.where(lane // moves == k, block, extra)
+    slot = extra[0:1]
+    slot_col = lax.broadcasted_iota(jnp.int32, (slots, LANES), 0).astype(F32)
+    hit = (slot_col == slot).astype(F32).astype(BF16)
+    taken = pick(jnp.concatenate([first_recv[origin[k]] for k in range(6)], axis=0), hit)
+    got = jnp.zeros((8, LANES), F32)
+    for k in range(6):
+        got = jnp.where(lane // moves == k, taken[8 * k : 8 * k + 8], got)
+    return got, extra, hit
+
+
+def induced_kernel(sizes, slots, moves, prepare):
     boxes = shell(sizes)
     images = image_list(boxes)
-
-    def kernel(recv, frames, ahi, alo, bhi, blo, own, perm, send, shift, lhs):
-        places = around(own_cell(), CENTERS[0], boxes, sizes)
+    length = box_length(slots) / CUTOFF
+
+    def kernel(recv, frames, ahi, alo, bhi, blo, own, perm, *rest):
+        if prepare:
+            first_recv, send, shift, arrive, hits, targets, lhs = rest
+        else:
+            send, shift, lhs = rest
+        cell = own_cell()
+        places = around(cell, CENTERS[0], boxes, sizes)
         build_lhs(lhs, recv, frames, places, images, slots)
         tensor = product(lhs, ahi, alo, slice(0, len(images) * slots))
         plain = product(lhs, bhi, blo, slice(0, len(boxes) * slots))
         rows = induced_rows(tensor, plain, own, perm, slots)
         shift[...] = jnp.concatenate([own[14:15] * row for row in rows], axis=0)
         send_moments(send, [own[13:14] * row for row in rows], slots)
+        if prepare:
+            origin = [linear(cell, [-step for step in unit], sizes) for unit in UNITS]
+            got, extra, hit = arrival_records(first_recv, origin, moves, slots)
+            arrive[0:8] = got
+            arrive[8:16] = extra
+            hits[...] = hit
+            slot = extra[0:1]
+            fr, root, part = derived(got[0:3], jnp.where(slot >= 0.0, got[4:5], -1.0), got[5:6], length)
+            cols = columns(jnp.concatenate([fr, root, part, got[6:7], slot, slot], axis=0))
+            for k in range(6):
+                for c, value in enumerate(target_of(cols[k * moves : (k + 1) * moves], length, 7)[0]):
+                    targets[k, c] = value
 
     return kernel
 
@@ -378,8 +430,8 @@
     length = edge / CUTOFF
 
     def kernel(
-        recv, frames, ahi, alo, bhi, blo, own, perm, shift, first_recv, source,
-        staying, arrivals, lhs, sums, acc, targets, table, out_stay, out_come, out_sems,
+        recv, frames, ahi, alo, bhi, blo, own, perm, shift, source, arrive, hits, targets,
+        staying, arrivals, lhs, sums, acc, table, out_stay, out_come, out_sems,
     ):
         cell = own_cell()
         places = around(cell, CENTERS[0], boxes, sizes)
@@ -387,38 +439,21 @@
         fill_table(table, cell, boxes, sizes)
         lane = lax.broadcasted_iota(jnp.int32, (1, LANES), 1)
         origin = [linear(cell, [-step for step in unit], sizes) for unit in UNITS]
-        extra = jnp.full((8, LANES), -1.0, F32)
-        for k in range(6):
-            side = (k % 2) * LANES
-            row = first_recv[origin[k], 7:8, side : side + LANES]
-            row = jnp.broadcast_to(row, (8, LANES))
-            fields = [pltpu.roll(row, (k * moves - c * moves) % LANES, 1)[0:1] for c in range(5)]
-            block = jnp.concatenate(fields + [extra[0:3]], axis=0)
-            extra = jnp.where(lane // moves == k, block, extra)
-        slot = extra[0:1]
-        slot_col = lax.broadcasted_iota(jnp.int32, (slots, LANES), 0).astype(F32)
-        hit = (slot_col == slot).astype(F32).astype(BF16)
         blank = jnp.zeros((5, slots), F32)
         blocks = []
         for k in range(6):
-            blocks.append(first_recv[origin[k]])
             for a in range(3):
                 blocks.append(
                     jnp.concatenate([recv[origin[k], a * halves + h] for h in range(halves)], axis=1)
                 )
             blocks.append(blank)
-        taken = pick(jnp.concatenate(blocks, axis=0), hit)
-        got = jnp.zeros((8, LANES), F32)
+        taken = pick(jnp.concatenate(blocks, axis=0), hits[...])
         moment = jnp.zeros((8, LANES), F32)
         for k in range(6):
-            got = jnp.where(lane // moves == k, taken[16 * k : 16 * k + 8], got)
-            moment = jnp.where(lane // moves == k, taken[16 * k + 8 : 16 * k + 16], moment)
-        present = slot >= 0.0
-        fr, root, part = derived(got[0:3], jnp.where(present, got[4:5], -1.0), got[5:6], length)
-        cols = columns(jnp.concatenate([fr, root, part, got[6:7], slot, slot], axis=0))
-        for k in range(6):
-            for c, value in enumerate(target_of(cols[k * tile : (k + 1) * tile], length, 7)[0]):
-                targets[k, c] = value
+            moment = jnp.where(lane // moves == k, taken[8 * k : 8 * k + 8], moment)
+        got = arrive[0:8]
+        extra = arrive[8:16]
+        present = extra[0:1] >= 0.0
         acc[...] = jnp.zeros(acc.shape, F32)
         steps = [len(images) // 6 * slots, len(boxes) // 6 * slots]
         for which, (high, low, count) in enumerate(((ahi, alo, len(images)), (bhi, blo, len(boxes)))):
@@ -563,7 +598,8 @@
             [
                 VMEM((padded_boxes, 8, slots), F32),
                 VMEM((slots, padded_boxes * 8), F32),
-                VMEM((3, 32, slots), F32),
+                VMEM((3, 8, slots), F32),
+                VMEM((7, 32, LANES), F32),
             ],
             1 << 25,
             8 << 20,
@@ -571,27 +607,30 @@
         got = exchange(moments)
         tensors = (frames, ahi, alo, bhi, blo, own, perm)
         lhs = VMEM((48, count_images * slots), BF16)
-        for _ in range(ITERS - 1):
-            moments, shift = call(
-                induced_kernel(sizes, slots),
-                [vmem()] * 8,
-                (shape(*moment_shape), shape(3, slots)),
-                (vmem(),) * 2,
+        for step in range(ITERS - 1):
+            prepare = step == ITERS - 2
+            outs = (shape(*moment_shape), shape(3, slots))
+            if prepare:
+                outs = outs + (shape(16, LANES), half(slots, LANES), shape(6, 7, moves, LANES))
+            moments, shift, *arriving = call(
+                induced_kernel(sizes, slots, moves, prepare),
+                [vmem()] * (9 if prepare else 8),
+                outs,
+                (vmem(),) * len(outs),
                 [lhs],
                 1 << 24,
                 4 << 20,
-            )(got, *tensors)
+            )(got, *tensors, *((first,) if prepare else ()))
             got = exchange(moments)
         staying, arrivals = call(
             final_kernel(sizes, slots, moves),
-            [vmem()] * 11,
+            [vmem()] * 13,
             (pltpu.HBM((9, 1, slots), F32), pltpu.HBM((14, 1, 6 * moves), F32)),
             (anywhere(), anywhere()),
             [
                 lhs,
                 VMEM((2, 48, slots), F32),
                 VMEM((3, LANES, LANES), F32),
-                VMEM((6, 7, moves, LANES), F32),
                 pltpu.SMEM((len(CENTERS) * count_boxes,), jnp.int32),
                 VMEM((9, 1, slots), F32),
                 VMEM((14, 1, 6 * moves), F32),
@@ -599,7 +638,7 @@
             ],
             1 << 24,
             8 << 20,
-        )(got, *tensors, shift, first, source)
+        )(got, *tensors, shift, source, *arriving)
         return staying.reshape(1, 1, 1, 9, slots), arrivals.reshape(1, 1, 1, 14, 6 * moves)
 
     box = P("gx", "gy", "gz", None)

time: 68.7 us -> 68.4 us (level)
  no operation moved by 1% of the time
where the time goes in v3:
time: 68.4 us; the launch traced here: 68.1 us
  blocking collectives  46.1 us (67%)
  Pallas kernels  20.8 us (30%)
  between operations  1.3 us (2%)
    all_to_all x4, blocking collectives, local(): exchange = lambda block: lax.all_to_all(block, AXES, 0, 0)  46.1 us
    pallas_call x1, Pallas kernels, local(): call(field_kernel(sizes, slots, 32), [vmem()] * 2, outs, (vmem(),) * len(...  9.87 us
    pallas_call x1, Pallas kernels, local(): call(final_kernel(sizes, slots, moves), [vmem()] * 13, (pltpu.HBM((9, 1,...  5.26 us
    pallas_call x2, Pallas kernels, local(): call(induced_kernel(sizes, slots, moves, prepare), [vmem()] * (9 if prepa...  4.36 us

profile of v3, /device:TPU:0, one launch (start us, length us, event | category | flops | bytes accessed | tf_op | source)
XLA Modules:
  0.0 68.1 jit_solution(17162734437439181470)
XLA Ops:
  1.3 1.3 %shard_map.104 = (f32[32,8,256]{2,1,0:T(8,128)S(1)}, f32[16,256]{1,0:T(8,128)S(1)}) custom-call(s32[1]{0:T(128)} %bitcast.15.refs_0_, f32[3,1,256]{2,1,0:T(1,128)} %bitcast.16, f32[3,1,256]{2,1,0:T(1,128)} %bitcast.17, f32[1,256]{1,0:T(1,128)} %bitcast.19, f32[1,256]{1,0:T(1,128)} %bitcast.20, f32[1,256]{1,0:T(1,128)} %bitcast.21, s32[1,256]{1,0:T(1,128)} %bitcast.22, ...), custom_call_target="tpu_custom_call" | custom-call | flops 1048576 | bytes 1048576 | tf_op jit(solution)/shard_map/pallas_call | solution.py:573
  2.6 17.6 %all_to_all.20.recv.rest_0_ = f32[32,8,256]{2,1,0:T(8,128)S(1)} all-to-all(f32[32,8,256]{2,1,0:T(8,128)S(1)} %get-tuple-element.20), channel_id=1, replica_groups=mesh['gx'=4,'gy'=4,'gz'=2] {'gx','gy','gz'}, dimensions={0} | all-to-all | bytes 524288 | tf_op jit(solution)/shard_map/all_to_all | solution.py:545
  20.2 9.9 %shard_map.105 = (f32[32,8,256]{2,1,0:T(8,128)S(1)}, f32[27,8,256]{2,1,0:T(8,128)S(1)}, bf16[6912,256]{1,0:T(8,128)(2,1)S(1)}, bf16[6912,256]{1,0:T(8,128)(2,1)S...) custom-call(f32[32,8,256]{2,1,0:T(8,128)S(1)} %all_to_all.20.recv.re, ...), custom_call_target="tpu_custom_call" | custom-call | flops 33554432 | bytes 1048576 | tf_op jit(solution)/shard_map/pallas_call | solution.py:593
  30.0 9.9 %all_to_all.21.recv = f32[32,6,1,128]{3,2,1,0:T(1,128)S(1)} all-to-all(f32[32,6,1,128]{3,2,1,0:T(1,128)S(1)} %get-tuple-element.22), channel_id=1, replica_groups=mesh['gx'=4,'gy'=4,'gz'=2] {'gx','gy','gz'}, dimensions={0} | all-to-all | bytes 196608 | tf_op jit(solution)/shard_map/all_to_all | solution.py:545
  40.0 2.4 %shard_map.106 = (f32[32,6,1,128]{3,2,1,0:T(1,128)S(1)}, f32[3,256]{1,0:T(4,128)}) custom-call(f32[32,6,1,128]{3,2,1,0:T(1,128)S(1)} %all_to_all.21.recv, f32[27,8,256]{2,1,0:T(8,128)S(1)} %get-tuple-element.23.frames, bf16[6912,256]{1,0:T(8,128)(2,1)S(1)} %get-tuple-element.24.ahi, bf16[6912,256]{1,0:T(8,128)(2,1)S(1)} %get-tuple-element.25.alo, ...), custom_call_target="tpu_custom_call" | custom-call | flops 16777216 | bytes 1048576 | tf_op jit(solution)/shard_map/pallas_call | solution.py:615
  42.3 9.3 %all_to_all.22.recv = f32[32,6,1,128]{3,2,1,0:T(1,128)S(1)} all-to-all(f32[32,6,1,128]{3,2,1,0:T(1,128)S(1)} %get-tuple-element.29), channel_id=1, replica_groups=mesh['gx'=4,'gy'=4,'gz'=2] {'gx','gy','gz'}, dimensions={0} | all-to-all | bytes 196608 | tf_op jit(solution)/shard_map/all_to_all | solution.py:545
  51.6 2.0 %shard_map.107 = (f32[32,6,1,128]{3,2,1,0:T(1,128)S(1)}, f32[3,256]{1,0:T(4,128)S(1)}, f32[16,128]{1,0:T(8,128)S(1)}, bf16[256,128]{1,0:T(8,128)(2,1)S(1)}, f32[6,7,16,128]{3,2,1,0:T(8,128)S(1)}) custom-call(f32[32,6,1,128]{3,2,1,0:T(1,128)S(1)} %all_to_all.22.recv, f32[27,8,256]{2,1,0:T(8,128)S(1)} %get-tuple-element.23.frames, ...), custom_call_target="tpu_custom_call" | custom-call | flops 16777216 | bytes 1048576 | tf_op jit(solution)/shard_map/pallas_call | solution.py:615
  53.6 9.3 %all_to_all.23.recv = f32[32,6,1,128]{3,2,1,0:T(1,128)S(1)} all-to-all(f32[32,6,1,128]{3,2,1,0:T(1,128)S(1)} %get-tuple-element.30), channel_id=1, replica_groups=mesh['gx'=4,'gy'=4,'gz'=2] {'gx','gy','gz'}, dimensions={0} | all-to-all | bytes 196608 | tf_op jit(solution)/shard_map/all_to_all | solution.py:545
  62.9 5.3 %shard_map.108 = (f32[9,1,256]{2,1,0:T(1,128)}, f32[14,1,96]{2,1,0:T(1,128)}) custom-call(f32[32,6,1,128]{3,2,1,0:T(1,128)S(1)} %all_to_all.23.recv, f32[27,8,256]{2,1,0:T(8,128)S(1)} %get-tuple-element.23.frames, bf16[6912,256]{1,0:T(8,128)(2,1)S(1)} %get-tuple-element.24.ahi, bf16[6912,256]{1,0:T(8,128)(2,1)S(1)} %get-tuple-element.25.alo, ...), custom_call_target="tpu_custom_call" | custom-call | flops 16777216 | bytes 1048576 | tf_op jit(solution)/shard_map/pallas_call | solution.py:625

commit v4 on v3

--- a/solution.py
+++ b/solution.py
@@ -285,7 +285,7 @@
                     fields[a] + jnp.sum((weight * deltas[a]).reshape(tile // 8, 8, slots), axis=0)
                     for a in range(3)
                 ]
-                radial = base * (inverse * inverse) * (tanh - half_x * (1.0 - tanh))
+                radial = (inverse * inverse) * (direct - half_x * (base - direct))
                 if is_center(box):
                     direct = jnp.where(keep, direct, 0.0)
                     radial = jnp.where(keep, radial, 0.0)
@@ -485,7 +485,7 @@
                         dist_sq = jnp.where(keep, dist_sq, 1.0)
                     inverse, half_x, tanh, base = terms(wide, dist_sq, row)
                     direct = base * tanh
-                    radial = base * (inverse * inverse) * (tanh - half_x * (1.0 - tanh))
+                    radial = (inverse * inverse) * (direct - half_x * (base - direct))
                     if is_center(box):
                         direct = jnp.where(keep, direct, 0.0)
                         radial = jnp.where(keep, radial, 0.0)

time: 68.4 us -> 68.2 us (level)
  no operation moved by 1% of the time
where the time goes in v4:
time: 68.2 us; the launch traced here: 67.9 us
  blocking collectives  46.1 us (68%)
  Pallas kernels  20.5 us (30%)
  between operations  1.3 us (2%)
    all_to_all x4, blocking collectives, local(): exchange = lambda block: lax.all_to_all(block, AXES, 0, 0)  46.1 us
    pallas_call x1, Pallas kernels, local(): call(field_kernel(sizes, slots, 32), [vmem()] * 2, outs, (vmem(),) * len(...  9.64 us
    pallas_call x1, Pallas kernels, local(): call(final_kernel(sizes, slots, moves), [vmem()] * 13, (pltpu.HBM((9, 1,...  5.25 us
    pallas_call x2, Pallas kernels, local(): call(induced_kernel(sizes, slots, moves, prepare), [vmem()] * (9 if prepa...  4.36 us

profile of v4, /device:TPU:0, one launch (start us, length us, event | category | flops | bytes accessed | tf_op | source)
XLA Modules:
  0.0 67.9 jit_solution(2296043586680836932)
XLA Ops:
  1.3 1.3 %shard_map.104 = (f32[32,8,256]{2,1,0:T(8,128)S(1)}, f32[16,256]{1,0:T(8,128)S(1)}) custom-call(s32[1]{0:T(128)} %bitcast.15.refs_0_, f32[3,1,256]{2,1,0:T(1,128)} %bitcast.16, f32[3,1,256]{2,1,0:T(1,128)} %bitcast.17, f32[1,256]{1,0:T(1,128)} %bitcast.19, f32[1,256]{1,0:T(1,128)} %bitcast.20, f32[1,256]{1,0:T(1,128)} %bitcast.21, s32[1,256]{1,0:T(1,128)} %bitcast.22, ...), custom_call_target="tpu_custom_call" | custom-call | flops 1048576 | bytes 1048576 | tf_op jit(solution)/shard_map/pallas_call | solution.py:573
  2.6 17.6 %all_to_all.20.recv.rest_0_ = f32[32,8,256]{2,1,0:T(8,128)S(1)} all-to-all(f32[32,8,256]{2,1,0:T(8,128)S(1)} %get-tuple-element.20), channel_id=1, replica_groups=mesh['gx'=4,'gy'=4,'gz'=2] {'gx','gy','gz'}, dimensions={0} | all-to-all | bytes 524288 | tf_op jit(solution)/shard_map/all_to_all | solution.py:545
  20.2 9.6 %shard_map.105 = (f32[32,8,256]{2,1,0:T(8,128)S(1)}, f32[27,8,256]{2,1,0:T(8,128)S(1)}, bf16[6912,256]{1,0:T(8,128)(2,1)S(1)}, bf16[6912,256]{1,0:T(8,128)(2,1)S...) custom-call(f32[32,8,256]{2,1,0:T(8,128)S(1)} %all_to_all.20.recv.re, ...), custom_call_target="tpu_custom_call" | custom-call | flops 33554432 | bytes 1048576 | tf_op jit(solution)/shard_map/pallas_call | solution.py:593
  29.8 9.9 %all_to_all.21.recv = f32[32,6,1,128]{3,2,1,0:T(1,128)S(1)} all-to-all(f32[32,6,1,128]{3,2,1,0:T(1,128)S(1)} %get-tuple-element.22), channel_id=1, replica_groups=mesh['gx'=4,'gy'=4,'gz'=2] {'gx','gy','gz'}, dimensions={0} | all-to-all | bytes 196608 | tf_op jit(solution)/shard_map/all_to_all | solution.py:545
  39.7 2.4 %shard_map.106 = (f32[32,6,1,128]{3,2,1,0:T(1,128)S(1)}, f32[3,256]{1,0:T(4,128)}) custom-call(f32[32,6,1,128]{3,2,1,0:T(1,128)S(1)} %all_to_all.21.recv, f32[27,8,256]{2,1,0:T(8,128)S(1)} %get-tuple-element.23.frames, bf16[6912,256]{1,0:T(8,128)(2,1)S(1)} %get-tuple-element.24.ahi, bf16[6912,256]{1,0:T(8,128)(2,1)S(1)} %get-tuple-element.25.alo, ...), custom_call_target="tpu_custom_call" | custom-call | flops 16777216 | bytes 1048576 | tf_op jit(solution)/shard_map/pallas_call | solution.py:615
  42.1 9.3 %all_to_all.22.recv = f32[32,6,1,128]{3,2,1,0:T(1,128)S(1)} all-to-all(f32[32,6,1,128]{3,2,1,0:T(1,128)S(1)} %get-tuple-element.29), channel_id=1, replica_groups=mesh['gx'=4,'gy'=4,'gz'=2] {'gx','gy','gz'}, dimensions={0} | all-to-all | bytes 196608 | tf_op jit(solution)/shard_map/all_to_all | solution.py:545
  51.4 2.0 %shard_map.107 = (f32[32,6,1,128]{3,2,1,0:T(1,128)S(1)}, f32[3,256]{1,0:T(4,128)S(1)}, f32[16,128]{1,0:T(8,128)S(1)}, bf16[256,128]{1,0:T(8,128)(2,1)S(1)}, f32[6,7,16,128]{3,2,1,0:T(8,128)S(1)}) custom-call(f32[32,6,1,128]{3,2,1,0:T(1,128)S(1)} %all_to_all.22.recv, f32[27,8,256]{2,1,0:T(8,128)S(1)} %get-tuple-element.23.frames, ...), custom_call_target="tpu_custom_call" | custom-call | flops 16777216 | bytes 1048576 | tf_op jit(solution)/shard_map/pallas_call | solution.py:615
  53.4 9.3 %all_to_all.23.recv = f32[32,6,1,128]{3,2,1,0:T(1,128)S(1)} all-to-all(f32[32,6,1,128]{3,2,1,0:T(1,128)S(1)} %get-tuple-element.30), channel_id=1, replica_groups=mesh['gx'=4,'gy'=4,'gz'=2] {'gx','gy','gz'}, dimensions={0} | all-to-all | bytes 196608 | tf_op jit(solution)/shard_map/all_to_all | solution.py:545
  62.6 5.3 %shard_map.108 = (f32[9,1,256]{2,1,0:T(1,128)}, f32[14,1,96]{2,1,0:T(1,128)}) custom-call(f32[32,6,1,128]{3,2,1,0:T(1,128)S(1)} %all_to_all.23.recv, f32[27,8,256]{2,1,0:T(8,128)S(1)} %get-tuple-element.23.frames, bf16[6912,256]{1,0:T(8,128)(2,1)S(1)} %get-tuple-element.24.ahi, bf16[6912,256]{1,0:T(8,128)(2,1)S(1)} %get-tuple-element.25.alo, ...), custom_call_target="tpu_custom_call" | custom-call | flops 16777216 | bytes 1048576 | tf_op jit(solution)/shard_map/pallas_call | solution.py:625

commit v5 on v4

--- a/solution.py
+++ b/solution.py
@@ -308,7 +308,7 @@
         for c in range(7):
             ready[c] = jnp.broadcast_to(cols[0:tile, c : c + 1], (tile, LANES))
 
-        lax.fori_loop(0, slots // tile, body, 0)
+        lax.fori_loop(0, slots // tile, body, 0, unroll=2)
         rows = [jnp.sum(acc[a], axis=0, keepdims=True) for a in range(3)]
         perm[...] = jnp.concatenate(rows, axis=0)
         send_moments(send, [own[13:14] * row for row in rows], slots)
@@ -602,7 +602,7 @@
                 VMEM((7, 32, LANES), F32),
             ],
             1 << 25,
-            8 << 20,
+            16 << 20,
         )(first, own)
         got = exchange(moments)
         tensors = (frames, ahi, alo, bhi, blo, own, perm)

time: 68.2 us -> 67.7 us (level)
  no operation moved by 1% of the time
where the time goes in v5:
time: 67.7 us; the launch traced here: 67.5 us
  blocking collectives  46 us (68%)
  Pallas kernels  20.1 us (30%)
  between operations  1.3 us (2%)
    all_to_all x4, blocking collectives, local(): exchange = lambda block: lax.all_to_all(block, AXES, 0, 0)  46 us
    pallas_call x1, Pallas kernels, local(): call(field_kernel(sizes, slots, 32), [vmem()] * 2, outs, (vmem(),) * len(...  9.18 us
    pallas_call x1, Pallas kernels, local(): call(final_kernel(sizes, slots, moves), [vmem()] * 13, (pltpu.HBM((9, 1,...  5.23 us
    pallas_call x2, Pallas kernels, local(): call(induced_kernel(sizes, slots, moves, prepare), [vmem()] * (9 if prepa...  4.4 us

profile of v5, /device:TPU:0, one launch (start us, length us, event | category | flops | bytes accessed | tf_op | source)
XLA Modules:
  0.0 67.5 jit_solution(4548173940299535329)
XLA Ops:
  1.3 1.3 %shard_map.104 = (f32[32,8,256]{2,1,0:T(8,128)S(1)}, f32[16,256]{1,0:T(8,128)S(1)}) custom-call(s32[1]{0:T(128)} %bitcast.15.refs_0_, f32[3,1,256]{2,1,0:T(1,128)} %bitcast.16, f32[3,1,256]{2,1,0:T(1,128)} %bitcast.17, f32[1,256]{1,0:T(1,128)} %bitcast.19, f32[1,256]{1,0:T(1,128)} %bitcast.20, f32[1,256]{1,0:T(1,128)} %bitcast.21, s32[1,256]{1,0:T(1,128)} %bitcast.22, ...), custom_call_target="tpu_custom_call" | custom-call | flops 1048576 | bytes 1048576 | tf_op jit(solution)/shard_map/pallas_call | solution.py:573
  2.6 17.6 %all_to_all.20.recv.rest_0_ = f32[32,8,256]{2,1,0:T(8,128)S(1)} all-to-all(f32[32,8,256]{2,1,0:T(8,128)S(1)} %get-tuple-element.20), channel_id=1, replica_groups=mesh['gx'=4,'gy'=4,'gz'=2] {'gx','gy','gz'}, dimensions={0} | all-to-all | bytes 524288 | tf_op jit(solution)/shard_map/all_to_all | solution.py:545
  20.2 9.2 %shard_map.105 = (f32[32,8,256]{2,1,0:T(8,128)S(1)}, f32[27,8,256]{2,1,0:T(8,128)S(1)}, bf16[6912,256]{1,0:T(8,128)(2,1)S(1)}, bf16[6912,256]{1,0:T(8,128)(2,1)S...) custom-call(f32[32,8,256]{2,1,0:T(8,128)S(1)} %all_to_all.20.recv.re, ...), custom_call_target="tpu_custom_call" | custom-call | flops 33554432 | bytes 1048576 | tf_op jit(solution)/shard_map/pallas_call | solution.py:593
  29.3 9.9 %all_to_all.21.recv = f32[32,6,1,128]{3,2,1,0:T(1,128)S(1)} all-to-all(f32[32,6,1,128]{3,2,1,0:T(1,128)S(1)} %get-tuple-element.22), channel_id=1, replica_groups=mesh['gx'=4,'gy'=4,'gz'=2] {'gx','gy','gz'}, dimensions={0} | all-to-all | bytes 196608 | tf_op jit(solution)/shard_map/all_to_all | solution.py:545
  39.3 2.4 %shard_map.106 = (f32[32,6,1,128]{3,2,1,0:T(1,128)S(1)}, f32[3,256]{1,0:T(4,128)}) custom-call(f32[32,6,1,128]{3,2,1,0:T(1,128)S(1)} %all_to_all.21.recv, f32[27,8,256]{2,1,0:T(8,128)S(1)} %get-tuple-element.23.frames, bf16[6912,256]{1,0:T(8,128)(2,1)S(1)} %get-tuple-element.24.ahi, bf16[6912,256]{1,0:T(8,128)(2,1)S(1)} %get-tuple-element.25.alo, ...), custom_call_target="tpu_custom_call" | custom-call | flops 16777216 | bytes 1048576 | tf_op jit(solution)/shard_map/pallas_call | solution.py:615
  41.7 9.3 %all_to_all.22.recv = f32[32,6,1,128]{3,2,1,0:T(1,128)S(1)} all-to-all(f32[32,6,1,128]{3,2,1,0:T(1,128)S(1)} %get-tuple-element.29), channel_id=1, replica_groups=mesh['gx'=4,'gy'=4,'gz'=2] {'gx','gy','gz'}, dimensions={0} | all-to-all | bytes 196608 | tf_op jit(solution)/shard_map/all_to_all | solution.py:545
  50.9 2.0 %shard_map.107 = (f32[32,6,1,128]{3,2,1,0:T(1,128)S(1)}, f32[3,256]{1,0:T(4,128)S(1)}, f32[16,128]{1,0:T(8,128)S(1)}, bf16[256,128]{1,0:T(8,128)(2,1)S(1)}, f32[6,7,16,128]{3,2,1,0:T(8,128)S(1)}) custom-call(f32[32,6,1,128]{3,2,1,0:T(1,128)S(1)} %all_to_all.22.recv, f32[27,8,256]{2,1,0:T(8,128)S(1)} %get-tuple-element.23.frames, ...), custom_call_target="tpu_custom_call" | custom-call | flops 16777216 | bytes 1048576 | tf_op jit(solution)/shard_map/pallas_call | solution.py:615
  52.9 9.3 %all_to_all.23.recv = f32[32,6,1,128]{3,2,1,0:T(1,128)S(1)} all-to-all(f32[32,6,1,128]{3,2,1,0:T(1,128)S(1)} %get-tuple-element.30), channel_id=1, replica_groups=mesh['gx'=4,'gy'=4,'gz'=2] {'gx','gy','gz'}, dimensions={0} | all-to-all | bytes 196608 | tf_op jit(solution)/shard_map/all_to_all | solution.py:545
  62.2 5.2 %shard_map.108 = (f32[9,1,256]{2,1,0:T(1,128)}, f32[14,1,96]{2,1,0:T(1,128)}) custom-call(f32[32,6,1,128]{3,2,1,0:T(1,128)S(1)} %all_to_all.23.recv, f32[27,8,256]{2,1,0:T(8,128)S(1)} %get-tuple-element.23.frames, bf16[6912,256]{1,0:T(8,128)(2,1)S(1)} %get-tuple-element.24.ahi, bf16[6912,256]{1,0:T(8,128)(2,1)S(1)} %get-tuple-element.25.alo, ...), custom_call_target="tpu_custom_call" | custom-call | flops 16777216 | bytes 1048576 | tf_op jit(solution)/shard_map/pallas_call | solution.py:625
